TPU v7x, 256 devices: a whole 4x4x8 slice. The times are simulated.
256 devices in a mesh: sec: 16 (over y, x), pair: 16 (over z, core).
Axes of the slice: x: 4, y: 4, z: 8, core: 2. Of those that a mesh axis runs over, the one named last changes fastest.
Arguments:
- left_ops: bfloat16 [16, 528, 256, 256], P('sec', 'pair'), may hold values from -6 to 6
- rotation: bfloat16 [16, 256, 128], P('sec'), may hold values from -0.375 to 0.375
- integrals: bfloat16 [528, 528], replicated, may hold values from -0.25 to 0.25
- right_ops: bfloat16 [16, 528, 128, 128], P('sec', 'pair'), may hold values from -0.001953125 to 0.001953125
- states: bfloat16 [16, 16, 128, 128], P('sec', None, 'pair'), may hold values from -6 to 6
- sector_sizes: int32 [16], P('sec'), may hold values from 32 to 128, as said below
- couplings: int32 [16, 4], P('sec'), may hold values from -1 to 15, as said below
- pair_order: int32 [528], replicated, may hold values from 0 to 527, each once
Outputs:
- sigma: float32 [16, 16, 128, 128], P('sec', None, 'pair')
Inputs may be any that keep to these rules, and one draw needn't show every extreme that they name: `sector_sizes`: some sector keeps all 128 states and some keeps 128 // 4. `couplings`: each row lists 1 to 4 distinct sectors in its first slots and -1 in the rest; some row is full and some lists one sector. `pair_order`: each pair appears once.
All inputs are finite; a program needn't handle non-finite values.
Results may differ from a plain program's by a relative error of at most 0.0064.
Values may be sent and summed in bfloat16 or wider, within the bound.
No kernel may reach another device: no remote copies, remote signals or barrier semaphores. Data moves between devices by JAX's collectives and lax.ppermute only.
A program may use at most 64 MiB of HBM per device.

v0:
```python
import functools

import jax
import jax.numpy as jnp
from jax import lax
from jax.experimental import pallas as pl
from jax.experimental.pallas import tpu as pltpu
from jax.sharding import Mesh
from jax.sharding import PartitionSpec as P


SEC = ("y", "x")
PAIR = ("z", "core")
FAR_FIRST = (4, 3, -3, 2, -2, 1, -1)
F32 = jnp.float32
BF16 = jnp.bfloat16
VMEM = pl.BlockSpec(memory_space=pltpu.VMEM)


def dot(a, b, dims):
    return lax.dot_general(a, b, (dims, ((), ())), preferred_element_type=F32)


def rotate_kernel(group, zs, rows, scalars, left, rotation, own, other, kept_ref, rows_ref):
    size, core = scalars[0], scalars[1]
    depth, width = rotation.shape

    @pl.when(pl.program_id(0) == 0)
    def _():
        live = lax.broadcasted_iota(jnp.int32, (depth, width), 1) < size
        kept = jnp.where(live, rotation[...].astype(F32), 0.0).astype(BF16)
        kept_ref[...] = kept
        slot = lax.broadcasted_iota(jnp.int32, (width, width), 0)
        target = lax.broadcasted_iota(jnp.int32, (width, width), 1)
        half = zs * rows
        which = (slot >= half).astype(jnp.int32)
        rest = slot - which * half
        place = core + which - 2 * core * which
        chip = lax.shift_right_logical(rest, 3)
        column = chip * (2 * rows) + place * rows + (rest - chip * rows)
        pick = jnp.where(column == target, 1.0, 0.0).astype(BF16)
        rows_ref[...] = dot(pick, kept, ((1,), (1,))).astype(BF16)

    kept = kept_ref[...]
    mine = rows_ref[...]
    flat = left[...].reshape(group * depth, depth)
    half = dot(flat, kept, ((1,), (0,))).astype(BF16)
    for g in range(group):
        result = dot(mine, half[g * depth : (g + 1) * depth], ((1,), (0,)))
        for chip in range(zs):
            own[chip, g] = result[chip * rows : (chip + 1) * rows].astype(BF16)
            low = (zs + chip) * rows
            other[chip, g] = result[low : low + rows].astype(BF16)


def rotate(left, rotation, scalars, zs, rows, group):
    pairs, depth, _ = left.shape
    width = rotation.shape[1]
    shape = jax.ShapeDtypeStruct((zs, pairs, rows, width), BF16)
    block = pl.BlockSpec((zs, group, rows, width), lambda g: (0, g, 0, 0))
    return pl.pallas_call(
        functools.partial(rotate_kernel, group, zs, rows),
        grid=(pairs // group,),
        in_specs=[
            pl.BlockSpec(memory_space=pltpu.SMEM),
            pl.BlockSpec((group, depth, depth), lambda g: (g, 0, 0)),
            pl.BlockSpec((depth, width), lambda g: (0, 0)),
        ],
        out_specs=[block, block],
        out_shape=[shape, shape],
        scratch_shapes=[pltpu.VMEM((depth, width), BF16), pltpu.VMEM((width, depth), BF16)],
    )(scalars, left, rotation)


def image_kernel(chunk, mixed, right, image):
    roots, width, _ = mixed.shape
    pairs = right.shape[0]

    def put(first, count):
        ops = right[pl.ds(first, count)].reshape(count * width, width)
        for start in range(0, roots, chunk):
            block = mixed[start : start + chunk].reshape(chunk * width, width)
            result = dot(block, ops, ((1,), (1,))).astype(BF16)
            for r in range(chunk):
                for j in range(count):
                    image[
                        pl.ds(pl.multiple_of((first + j) * width, width), width),
                        (start + r) * width : (start + r + 1) * width,
                    ] = result[r * width : (r + 1) * width, j * width : (j + 1) * width]

    def step(i, carry):
        put(2 * i, 2)
        return carry

    lax.fori_loop(0, pairs // 2, step, 0)
    if pairs % 2:
        put(pairs - 1, 1)


def make_image(mixed, right):
    roots, width, _ = mixed.shape
    pairs = right.shape[0]
    return pl.pallas_call(
        functools.partial(image_kernel, 4),
        in_specs=[VMEM, VMEM],
        out_specs=VMEM,
        out_shape=jax.ShapeDtypeStruct((pairs * width, roots * width), BF16),
    )(mixed, right)


def sigma_kernel(comp, image, total):
    pairs, width, _ = comp.shape
    tile = 256

    def step(n, carry):
        lanes = pl.ds(pl.multiple_of(n * tile, tile), tile)
        sums = jnp.zeros((width, tile), F32)
        for q in range(0, pairs - 1, 2):
            two = jnp.concatenate([comp[q], comp[q + 1]], axis=1)
            sums += dot(two, image[q * width : (q + 2) * width, lanes], ((1,), (0,)))
        if pairs % 2:
            sums += dot(comp[pairs - 1], image[(pairs - 1) * width : pairs * width, lanes], ((1,), (0,)))
        total[:, lanes] = sums
        return carry

    lax.fori_loop(0, image.shape[1] // tile, step, 0)


def make_sigma(comp, image):
    return pl.pallas_call(
        sigma_kernel,
        in_specs=[VMEM, VMEM],
        out_specs=VMEM,
        out_shape=jax.ShapeDtypeStruct((comp.shape[1], image.shape[1]), F32),
    )(comp, image)


def other_core(x):
    return lax.ppermute(x, "core", [(0, 1), (1, 0)])


def in_core_order(own, other, dim):
    first = lax.axis_index("core") == 0
    return jnp.where(
        first, jnp.stack([own, other], axis=dim), jnp.stack([other, own], axis=dim)
    )


def send_over_z(block_of):
    n = lax.axis_size("z")
    me = lax.axis_index("z")
    arrived = []
    for shift in FAR_FIRST:
        pairs = [(i, (i + shift) % n) for i in range(n)]
        block = block_of(lax.rem(me + (shift + n), n))
        arrived.append(lax.ppermute(block, "z", pairs))
    return arrived


def place_by_source(own, arrived):
    n = lax.axis_size("z")
    me = lax.axis_index("z")
    whole = lax.dynamic_update_slice_in_dim(jnp.zeros((n, *own.shape), own.dtype), own[None], me, 0)
    for shift, block in zip(FAR_FIRST, arrived):
        whole = lax.dynamic_update_slice_in_dim(whole, block[None], lax.rem(me + (n - shift), n), 0)
    return whole


def body(left_ops, rotation, integrals, right_ops, states, sector_sizes, couplings, pair_order):
    core = lax.axis_index("core")
    zs = lax.axis_size("z")
    cores = lax.axis_size("core")
    me = lax.axis_index("z")
    width = rotation.shape[2]
    pairs = left_ops.shape[1]
    roots, rows = states.shape[1], states.shape[2]
    sectors = lax.axis_size(SEC)
    all_pairs = integrals.shape[1]

    def flip(x):
        parts = x.reshape(zs, cores, pairs, *x.shape[1:])
        return jnp.where(core == 0, parts, parts[:, ::-1]).reshape(x.shape)

    scalars = jnp.stack([sector_sizes[0], core.astype(jnp.int32)])
    own, other = rotate(left_ops[0], rotation[0], scalars, zs, rows, 3)
    theirs = other_core(other)

    copies = jnp.broadcast_to(states, (sectors, *states.shape[1:]))
    sources = lax.all_to_all(copies, SEC, 0, 0, tiled=True)

    def rotated_block(chip):
        return jnp.concatenate(
            [
                lax.dynamic_index_in_dim(own, chip, 0, keepdims=False),
                lax.dynamic_index_in_dim(theirs, chip, 0, keepdims=False),
            ],
            axis=0,
        )

    arrived = send_over_z(rotated_block)
    rotated_all = place_by_source(rotated_block(me), arrived)
    rotated_all = rotated_all.reshape(all_pairs, rows, width)

    order = flip(pair_order)
    taken = (jnp.arange(all_pairs, dtype=jnp.int32)[:, None] == order[None, :]).astype(BF16)
    ordered = jnp.dot(flip(integrals), taken, preferred_element_type=F32).astype(BF16)
    ordered, rotated_all = lax.optimization_barrier((ordered, rotated_all))

    sector_ids = jnp.arange(sectors, dtype=jnp.int32)
    weights = jnp.sum((couplings[0][:, None] == sector_ids[None, :]).astype(F32), axis=0)
    mixed_rows = jnp.sum(
        weights[:, None, None, None] * sources.astype(F32), axis=0
    ).astype(BF16)
    copies = jnp.broadcast_to(mixed_rows[None], (zs, *mixed_rows.shape))
    mixed_z = lax.all_to_all(copies, "z", 0, 0, tiled=True)
    mixed_other = other_core(mixed_z)
    mixed = in_core_order(mixed_z, mixed_other, 1)
    mixed = mixed.transpose(2, 0, 1, 3, 4).reshape(roots, width, width)
    image = make_image(mixed, right_ops[0])

    comp = jnp.einsum("qi,iab->qab", ordered, rotated_all, preferred_element_type=F32).astype(BF16)
    comp = comp.reshape(zs, cores * pairs, rows, width)

    def comp_block(chip):
        return lax.dynamic_index_in_dim(comp, chip, 0, keepdims=False)

    arrived = send_over_z(comp_block)
    blocks = [comp_block(me)] + arrived
    mine = jnp.stack([b[:pairs] for b in blocks], axis=1)
    theirs = other_core(jnp.stack([b[pairs:] for b in blocks], axis=1))
    comp = jnp.concatenate([mine, theirs], axis=1).reshape(pairs, width, width)

    total = make_sigma(comp, image)
    total = total.reshape(cores, zs, rows, roots * width)
    theirs = other_core(total[1].astype(BF16))
    chip = (total[0] + theirs.astype(F32)).astype(BF16)

    place = {shift % zs: number + 1 for number, shift in enumerate(FAR_FIRST)}
    place[0] = 0
    by_shift = jnp.stack([chip[place[s]] for s in range(zs)])
    twice = jnp.concatenate([by_shift[::-1], by_shift[::-1]], axis=0)
    parts = lax.dynamic_slice_in_dim(twice, zs - 1 - me, zs, 0)
    parts = lax.all_to_all(parts, "z", 0, 0, tiled=True)
    result = parts.astype(F32).sum(axis=0)
    return result.reshape(rows, roots, width).transpose(1, 0, 2)[None]


def solution(mesh):
    torus = Mesh(mesh.devices.reshape(4, 4, -1, 2), ("y", "x", "z", "core"))
    placed = (
        P(SEC, PAIR, None, None),
        P(SEC, None, None),
        P(),
        P(SEC, PAIR, None, None),
        P(SEC, None, PAIR, None),
        P(SEC),
        P(SEC, None),
        P(),
    )
    return jax.shard_map(
        body, mesh=torus, in_specs=placed, out_specs=P(SEC, None, PAIR, None), check_vma=False
    )
```

profile of v0, /device:TPU:1, one launch (start us, length us, event | category | flops | bytes accessed | tf_op | source)
XLA Modules:
  0.0 161.7 jit_solution(4316821419624428714)
XLA Ops:
  0.0 1.7 %broadcast_in_dim.56 = bf16[16,16,8,128]{3,2,1,0:T(8,128)(2,1)} broadcast(bf16[16,8,128]{2,1,0:T(8,128)(2,1)} %bitcast.175), dimensions={1,2,3} | broadcast | bytes 557056 | tf_op jit(solution)/shard_map/broadcast_in_dim | solution.py:188
  1.7 7.6 %all-to-all-start = ((bf16[16,16,8,128]{3,2,1,0:T(8,128)(2,1)}), bf16[16,16,8,128]{3,2,1,0:T(8,128)(2,1)S(1)}, u32[]{:S(2)}, u32[]{:S(2)}) async-start(bf16[16,16,8,128]{3,2,1,0:T(8,128)(2,1)} %broadcast_in_dim.56), calls=%async_computation | async-start | bytes 1048576 | tf_op jit(solution)/shard_map/all_to_all | solution.py:189
  9.9 0.6 pad_add_fusion.scalars
  10.5 10.2 %shard_map.82 = (bf16[8,33,8,128]{3,2,1,0:T(8,128)(2,1)}, bf16[8,33,8,128]{3,2,1,0:T(8,128)(2,1)}) custom-call(s32[2]{0:T(128)} %pad_add_fusion.scalars, bf16[33,256,256]{2,1,0:T(8,128)(2,1)} %bitcast.165, bf16[256,128]{1,0:T(8,128)(2,1)} %bitcast.174), custom_call_target="tpu_custom_call" | custom-call | tf_op jit(solution)/shard_map/pallas_call | solution.py:61
  20.7 1.0 collective-permute-start
  22.3 0.3 reshape.41
  23.3 0.9 convolution_convert_fusion.1
  24.2 7.0 %collective-permute-start.1 = (bf16[66,8,128]{2,1,0:T(8,128)(2,1)S(1)}, bf16[66,8,128]{2,1,0:T(8,128)(2,1)S(1)}, u32[]{:S(2)}, u32[]{:S(2)}) collective-permute-start(bf16[66,8,128]{2,1,0:T(8,128)(2,1)S(1)} %pad_maximum_fusion), channel_id=1, source_target_pairs={{0,8},{2,10},{4,12},{6,14},{8,0},{10,2},{12,4},{14,6},{1,9},{3,11}... | collective-permute-start | bytes 405512 | tf_op jit(solution)/shard_map/ppermute | solution.py:156
  31.3 1.7 %collective-permute-start.2 = (bf16[66,8,128]{2,1,0:T(8,128)(2,1)S(1)}, bf16[66,8,128]{2,1,0:T(8,128)(2,1)S(1)}, u32[]{:S(2)}, u32[]{:S(2)}) collective-permute-start(bf16[66,8,128]{2,1,0:T(8,128)(2,1)S(1)} %pad_maximum_fusion.1), channel_id=1, source_target_pairs={{0,6},{2,8},{4,10},{6,12},{8,14},{10,0},{12,2},{14,4},{1,7},{3,9},... | collective-permute-start | bytes 405512 | tf_op jit(solution)/shard_map/ppermute | solution.py:156
  33.0 2.9 %collective-permute-start.3 = (bf16[66,8,128]{2,1,0:T(8,128)(2,1)S(1)}, bf16[66,8,128]{2,1,0:T(8,128)(2,1)S(1)}, u32[]{:S(2)}, u32[]{:S(2)}) collective-permute-start(bf16[66,8,128]{2,1,0:T(8,128)(2,1)S(1)} %pad_maximum_fusion.2), channel_id=1, source_target_pairs={{0,10},{2,12},{4,14},{6,0},{8,2},{10,4},{12,6},{14,8},{1,11},{3,13... | collective-permute-start | bytes 405512 | tf_op jit(solution)/shard_map/ppermute | solution.py:156
  35.9 1.3 collective-permute-start.4
  37.2 2.5 %collective-permute-start.5 = (bf16[66,8,128]{2,1,0:T(8,128)(2,1)S(1)}, bf16[66,8,128]{2,1,0:T(8,128)(2,1)S(1)}, u32[]{:S(2)}, u32[]{:S(2)}) collective-permute-start(bf16[66,8,128]{2,1,0:T(8,128)(2,1)S(1)} %pad_maximum_fusion.4), channel_id=1, source_target_pairs={{0,12},{2,14},{4,0},{6,2},{8,4},{10,6},{12,8},{14,10},{1,13},{3,15... | collective-permute-start | bytes 405512 | tf_op jit(solution)/shard_map/ppermute | solution.py:156
  39.9 0.8 collective-permute-start.6
  40.7 7.0 %collective-permute-done.2 = bf16[66,8,128]{2,1,0:T(8,128)(2,1)S(1)} collective-permute-done((bf16[66,8,128]{2,1,0:T(8,128)(2,1)S(1)}, bf16[66,8,128]{2,1,0:T(8,128)(2,1)S(1)}, u32[]{:S(2)}, u32[]{:S(2)}) %collective-permute-start.2) | collective-permute-done | bytes 135200 | tf_op jit(solution)/shard_map/ppermute | solution.py:156
  47.8 1.2 collective-permute-done.4
  49.0 3.8 %collective-permute-done.5 = bf16[66,8,128]{2,1,0:T(8,128)(2,1)S(1)} collective-permute-done((bf16[66,8,128]{2,1,0:T(8,128)(2,1)S(1)}, bf16[66,8,128]{2,1,0:T(8,128)(2,1)S(1)}, u32[]{:S(2)}, u32[]{:S(2)}) %collective-permute-start.5) | collective-permute-done | bytes 135200 | tf_op jit(solution)/shard_map/ppermute | solution.py:156
  52.9 2.3 %collective-permute-done.6 = bf16[66,8,128]{2,1,0:T(8,128)(2,1)S(1)} collective-permute-done((bf16[66,8,128]{2,1,0:T(8,128)(2,1)S(1)}, bf16[66,8,128]{2,1,0:T(8,128)(2,1)S(1)}, u32[]{:S(2)}, u32[]{:S(2)}) %collective-permute-start.6) | collective-permute-done | bytes 135200 | tf_op jit(solution)/shard_map/ppermute | solution.py:156
  55.3 0.7 collective-permute-done.7
  56.0 1.0 convolution_convert_fusion
  57.4 3.5 %collective-permute-start.8 = (bf16[66,8,128]{2,1,0:T(8,128)(2,1)S(1)}, bf16[66,8,128]{2,1,0:T(8,128)(2,1)S(1)}, u32[]{:S(2)}, u32[]{:S(2)}) collective-permute-start(bf16[66,8,128]{2,1,0:T(8,128)(2,1)S(1)} %get-tuple-element.21), channel_id=1, source_target_pairs={{0,8},{2,10},{4,12},{6,14},{8,0},{10,2},{12,4},{14,6},{1,9},{3,11}... | collective-permute-start | bytes 405512 | tf_op jit(solution)/shard_map/ppermute | solution.py:156
  61.1 0.7 broadcast_in_dim.57
  61.8 3.5 %all-to-all-start.1 = ((bf16[8,16,8,128]{3,2,1,0:T(8,128)(2,1)}), bf16[8,16,8,128]{3,2,1,0:T(8,128)(2,1)S(1)}, u32[]{:S(2)}, u32[]{:S(2)}) async-start(bf16[8,16,8,128]{3,2,1,0:T(8,128)(2,1)} %broadcast_in_dim.57), calls=%async_computation.1 | async-start | bytes 524288 | tf_op jit(solution)/shard_map/all_to_all | solution.py:215
  65.4 2.7 %collective-permute-start.14 = (bf16[66,8,128]{2,1,0:T(8,128)(2,1)S(1)}, bf16[66,8,128]{2,1,0:T(8,128)(2,1)S(1)}, u32[]{:S(2)}, u32[]{:S(2)}) collective-permute-start(bf16[66,8,128]{2,1,0:T(8,128)(2,1)S(1)} %get-tuple-element.15), channel_id=1, source_target_pairs={{0,14},{2,0},{4,2},{6,4},{8,6},{10,8},{12,10},{14,12},{1,15},{3,1}... | collective-permute-start | bytes 405512 | tf_op jit(solution)/shard_map/ppermute | solution.py:156
  68.0 2.4 %collective-permute-start.12 = (bf16[66,8,128]{2,1,0:T(8,128)(2,1)S(1)}, bf16[66,8,128]{2,1,0:T(8,128)(2,1)S(1)}, u32[]{:S(2)}, u32[]{:S(2)}) collective-permute-start(bf16[66,8,128]{2,1,0:T(8,128)(2,1)S(1)} %get-tuple-element.17), channel_id=1, source_target_pairs={{0,12},{2,14},{4,0},{6,2},{8,4},{10,6},{12,8},{14,10},{1,13},{3,15... | collective-permute-start | bytes 405512 | tf_op jit(solution)/shard_map/ppermute | solution.py:156
  70.4 0.6 fusion.16
  71.0 4.5 %collective-permute-start.9 = (bf16[66,8,128]{2,1,0:T(8,128)(2,1)S(1)}, bf16[66,8,128]{2,1,0:T(8,128)(2,1)S(1)}, u32[]{:S(2)}, u32[]{:S(2)}) collective-permute-start(bf16[66,8,128]{2,1,0:T(8,128)(2,1)S(1)} %get-tuple-element.20), channel_id=1, source_target_pairs={{0,6},{2,8},{4,10},{6,12},{8,14},{10,0},{12,2},{14,4},{1,7},{3,9},... | collective-permute-start | bytes 405512 | tf_op jit(solution)/shard_map/ppermute | solution.py:156
  75.5 0.6 fusion.15
  76.1 15.3 %collective-permute-done.9 = bf16[66,8,128]{2,1,0:T(8,128)(2,1)S(1)} collective-permute-done((bf16[66,8,128]{2,1,0:T(8,128)(2,1)S(1)}, bf16[66,8,128]{2,1,0:T(8,128)(2,1)S(1)}, u32[]{:S(2)}, u32[]{:S(2)}) %collective-permute-start.9) | collective-permute-done | bytes 135200 | tf_op jit(solution)/shard_map/ppermute | solution.py:156
  91.5 4.2 %collective-permute-start.10 = (bf16[66,8,128]{2,1,0:T(8,128)(2,1)S(1)}, bf16[66,8,128]{2,1,0:T(8,128)(2,1)S(1)}, u32[]{:S(2)}, u32[]{:S(2)}) collective-permute-start(bf16[66,8,128]{2,1,0:T(8,128)(2,1)S(1)} %get-tuple-element.19), channel_id=1, source_target_pairs={{0,10},{2,12},{4,14},{6,0},{8,2},{10,4},{12,6},{14,8},{1,11},{3,13... | collective-permute-start | bytes 405512 | tf_op jit(solution)/shard_map/ppermute | solution.py:156
  95.7 0.6 fusion.14
  96.3 4.8 %collective-permute-done.10 = bf16[66,8,128]{2,1,0:T(8,128)(2,1)S(1)} collective-permute-done((bf16[66,8,128]{2,1,0:T(8,128)(2,1)S(1)}, bf16[66,8,128]{2,1,0:T(8,128)(2,1)S(1)}, u32[]{:S(2)}, u32[]{:S(2)}) %collective-permute-start.10) | collective-permute-done | bytes 135200 | tf_op jit(solution)/shard_map/ppermute | solution.py:156
  101.1 0.6 fusion.13
  101.7 0.6 fusion.12
  102.4 0.6 fusion.11
  103.0 0.6 fusion.10
  103.7 0.6 fusion.9
  104.3 4.0 %collective-permute-start.15 = (bf16[33,8,8,128]{3,2,0,1:T(8,128)(2,1)}, bf16[33,8,8,128]{3,2,0,1:T(8,128)(2,1)S(1)}, u32[]{:S(2)}, u32[]{:S(2)}) collective-permute-start(bf16[33,8,8,128]{3,2,0,1:T(8,128)(2,1)} %get-tuple-element.38), channel_id=1, source_target_pairs={{0,1},{1,0},{2,3},{3,2},{4,5},{5,4},{6,7},{7,6},{8,9},{9,8},{10,11... | collective-permute-start | bytes 1622024 | tf_op jit(solution)/shard_map/ppermute | solution.py:139
  108.3 2.1 %collective-permute-done.16 = bf16[8,16,8,128]{3,2,1,0:T(8,128)(2,1)S(1)} collective-permute-done((bf16[8,16,8,128]{3,2,1,0:T(8,128)(2,1)S(1)}, bf16[8,16,8,128]{3,2,1,0:T(8,128)(2,1)S(1)}, u32[]{:S(2)}, u32[]{:S(2)}) %collective-permute-start.16) | collective-permute-done | bytes 262176 | tf_op jit(solution)/shard_map/ppermute | solution.py:139
  110.6 1.0 copy.35
  111.5 16.7 %shard_map.83.image = bf16[4224,2048]{1,0:T(8,128)(2,1)} custom-call(bf16[16,128,128]{2,1,0:T(8,128)(2,1)} %bitcast.168, bf16[33,128,128]{2,1,0:T(8,128)(2,1)} %bitcast.169), custom_call_target="tpu_custom_call" | custom-call | tf_op jit(solution)/shard_map/pallas_call | solution.py:103
  128.3 1.3 copy.39
  129.6 11.4 %shard_map.84 = f32[128,2048]{1,0:T(8,128)} custom-call(bf16[33,128,128]{2,1,0:T(8,128)(2,1)} %bitcast.164, bf16[4224,2048]{1,0:T(8,128)(2,1)} %shard_map.83.image), custom_call_target="tpu_custom_call" | custom-call | tf_op jit(solution)/shard_map/pallas_call | solution.py:130
  141.0 1.1 fusion.7
  142.1 0.5 collective-permute-start.17
  142.5 1.2 collective-permute-done.17
  143.7 1.1 fusion.4
  145.0 16.1 %all_to_all.15 = bf16[8,8,2048]{2,1,0:T(8,128)(2,1)S(1)} all-to-all(bf16[8,8,2048]{2,1,0:T(8,128)(2,1)S(1)} %fusion.6), channel_id=1, replica_groups=mesh['y'=4,'x'=4,'z'=8,'core'=2] {'z'}, dimensions={0} | all-to-all | bytes 524288 | tf_op jit(solution)/shard_map/all_to_all | solution.py:243
  161.1 0.7 convert_reduce_fusion
  (63 shorter events, 2.5 us)
Async XLA Ops:
  1.7 59.2 %all-to-all-start = ((bf16[16,16,8,128]{3,2,1,0:T(8,128)(2,1)}), bf16[16,16,8,128]{3,2,1,0:T(8,128)(2,1)S(1)}, u32[]{:S(2)}, u32[]{:S(2)}) async-start(bf16[16,16,8,128]{3,2,1,0:T(8,128)(2,1)} %broadcast_in_dim.56), calls=%async_computation | async-start | bytes 1048576 | tf_op jit(solution)/shard_map/all_to_all | solution.py:189
  10.5 11.1 %copy-start.2 = (s32[528]{0:T(1024)S(1)}, s32[528]{0:T(1024)}, u32[]{:S(2)}) copy-start(s32[528]{0:T(1024)} %param.15) | copy-start | bytes 6340
  10.5 11.3 %copy-start = (bf16[528,528]{1,0:T(8,128)(2,1)S(1)}, bf16[528,528]{1,0:T(8,128)(2,1)}, u32[]{:S(2)}) copy-start(bf16[528,528]{1,0:T(8,128)(2,1)} %param.10) | copy-start | bytes 1672708
  20.7 3.5 %collective-permute-start = (bf16[8,33,8,128]{3,2,1,0:T(8,128)(2,1)}, bf16[8,33,8,128]{3,2,1,0:T(8,128)(2,1)S(1)}, u32[]{:S(2)}, u32[]{:S(2)}) collective-permute-start(bf16[8,33,8,128]{3,2,1,0:T(8,128)(2,1)} %get-tuple-element.10), channel_id=1, source_target_pairs={{0,1},{1,0},{2,3},{3,2},{4,5},{5,4},{6,7},{7,6},{8,9},{9,8},{10,11... | collective-permute-start | bytes 1622024 | tf_op jit(solution)/shard_map/ppermute | solution.py:139
  22.2 0.7 copy-start.3
  22.2 1.1 copy-start.1
  24.2 15.7 %collective-permute-start.1 = (bf16[66,8,128]{2,1,0:T(8,128)(2,1)S(1)}, bf16[66,8,128]{2,1,0:T(8,128)(2,1)S(1)}, u32[]{:S(2)}, u32[]{:S(2)}) collective-permute-start(bf16[66,8,128]{2,1,0:T(8,128)(2,1)S(1)} %pad_maximum_fusion), channel_id=1, source_target_pairs={{0,8},{2,10},{4,12},{6,14},{8,0},{10,2},{12,4},{14,6},{1,9},{3,11}... | collective-permute-start | bytes 405512 | tf_op jit(solution)/shard_map/ppermute | solution.py:156
  31.3 16.4 %collective-permute-start.2 = (bf16[66,8,128]{2,1,0:T(8,128)(2,1)S(1)}, bf16[66,8,128]{2,1,0:T(8,128)(2,1)S(1)}, u32[]{:S(2)}, u32[]{:S(2)}) collective-permute-start(bf16[66,8,128]{2,1,0:T(8,128)(2,1)S(1)} %pad_maximum_fusion.1), channel_id=1, source_target_pairs={{0,6},{2,8},{4,10},{6,12},{8,14},{10,0},{12,2},{14,4},{1,7},{3,9},... | collective-permute-start | bytes 405512 | tf_op jit(solution)/shard_map/ppermute | solution.py:156
  33.0 14.7 %collective-permute-start.3 = (bf16[66,8,128]{2,1,0:T(8,128)(2,1)S(1)}, bf16[66,8,128]{2,1,0:T(8,128)(2,1)S(1)}, u32[]{:S(2)}, u32[]{:S(2)}) collective-permute-start(bf16[66,8,128]{2,1,0:T(8,128)(2,1)S(1)} %pad_maximum_fusion.2), channel_id=1, source_target_pairs={{0,10},{2,12},{4,14},{6,0},{8,2},{10,4},{12,6},{14,8},{1,11},{3,13... | collective-permute-start | bytes 405512 | tf_op jit(solution)/shard_map/ppermute | solution.py:156
  35.9 13.1 %collective-permute-start.4 = (bf16[66,8,128]{2,1,0:T(8,128)(2,1)S(1)}, bf16[66,8,128]{2,1,0:T(8,128)(2,1)S(1)}, u32[]{:S(2)}, u32[]{:S(2)}) collective-permute-start(bf16[66,8,128]{2,1,0:T(8,128)(2,1)S(1)} %pad_maximum_fusion.3), channel_id=1, source_target_pairs={{0,4},{2,6},{4,8},{6,10},{8,12},{10,14},{12,0},{14,2},{1,5},{3,7},... | collective-permute-start | bytes 405512 | tf_op jit(solution)/shard_map/ppermute | solution.py:156
  37.2 15.7 %collective-permute-start.5 = (bf16[66,8,128]{2,1,0:T(8,128)(2,1)S(1)}, bf16[66,8,128]{2,1,0:T(8,128)(2,1)S(1)}, u32[]{:S(2)}, u32[]{:S(2)}) collective-permute-start(bf16[66,8,128]{2,1,0:T(8,128)(2,1)S(1)} %pad_maximum_fusion.4), channel_id=1, source_target_pairs={{0,12},{2,14},{4,0},{6,2},{8,4},{10,6},{12,8},{14,10},{1,13},{3,15... | collective-permute-start | bytes 405512 | tf_op jit(solution)/shard_map/ppermute | solution.py:156
  39.9 15.3 %collective-permute-start.6 = (bf16[66,8,128]{2,1,0:T(8,128)(2,1)S(1)}, bf16[66,8,128]{2,1,0:T(8,128)(2,1)S(1)}, u32[]{:S(2)}, u32[]{:S(2)}) collective-permute-start(bf16[66,8,128]{2,1,0:T(8,128)(2,1)S(1)} %pad_maximum_fusion.5), channel_id=1, source_target_pairs={{0,2},{2,4},{4,6},{6,8},{8,10},{10,12},{12,14},{14,0},{1,3},{3,5},... | collective-permute-start | bytes 405512 | tf_op jit(solution)/shard_map/ppermute | solution.py:156
  47.7 8.3 %collective-permute-start.7 = (bf16[66,8,128]{2,1,0:T(8,128)(2,1)S(1)}, bf16[66,8,128]{2,1,0:T(8,128)(2,1)S(1)}, u32[]{:S(2)}, u32[]{:S(2)}) collective-permute-start(bf16[66,8,128]{2,1,0:T(8,128)(2,1)S(1)} %pad_maximum_fusion.6), channel_id=1, source_target_pairs={{0,14},{2,0},{4,2},{6,4},{8,6},{10,8},{12,10},{14,12},{1,15},{3,1}... | collective-permute-start | bytes 405512 | tf_op jit(solution)/shard_map/ppermute | solution.py:156
  57.4 13.6 %collective-permute-start.8 = (bf16[66,8,128]{2,1,0:T(8,128)(2,1)S(1)}, bf16[66,8,128]{2,1,0:T(8,128)(2,1)S(1)}, u32[]{:S(2)}, u32[]{:S(2)}) collective-permute-start(bf16[66,8,128]{2,1,0:T(8,128)(2,1)S(1)} %get-tuple-element.21), channel_id=1, source_target_pairs={{0,8},{2,10},{4,12},{6,14},{8,0},{10,2},{12,4},{14,6},{1,9},{3,11}... | collective-permute-start | bytes 405512 | tf_op jit(solution)/shard_map/ppermute | solution.py:156
  61.8 46.5 %all-to-all-start.1 = ((bf16[8,16,8,128]{3,2,1,0:T(8,128)(2,1)}), bf16[8,16,8,128]{3,2,1,0:T(8,128)(2,1)S(1)}, u32[]{:S(2)}, u32[]{:S(2)}) async-start(bf16[8,16,8,128]{3,2,1,0:T(8,128)(2,1)} %broadcast_in_dim.57), calls=%async_computation.1 | async-start | bytes 524288 | tf_op jit(solution)/shard_map/all_to_all | solution.py:215
  65.4 38.3 %collective-permute-start.14 = (bf16[66,8,128]{2,1,0:T(8,128)(2,1)S(1)}, bf16[66,8,128]{2,1,0:T(8,128)(2,1)S(1)}, u32[]{:S(2)}, u32[]{:S(2)}) collective-permute-start(bf16[66,8,128]{2,1,0:T(8,128)(2,1)S(1)} %get-tuple-element.15), channel_id=1, source_target_pairs={{0,14},{2,0},{4,2},{6,4},{8,6},{10,8},{12,10},{14,12},{1,15},{3,1}... | collective-permute-start | bytes 405512 | tf_op jit(solution)/shard_map/ppermute | solution.py:156
  68.0 35.0 %collective-permute-start.13 = (bf16[66,8,128]{2,1,0:T(8,128)(2,1)S(1)}, bf16[66,8,128]{2,1,0:T(8,128)(2,1)S(1)}, u32[]{:S(2)}, u32[]{:S(2)}) collective-permute-start(bf16[66,8,128]{2,1,0:T(8,128)(2,1)S(1)} %get-tuple-element.16), channel_id=1, source_target_pairs={{0,2},{2,4},{4,6},{6,8},{8,10},{10,12},{12,14},{14,0},{1,3},{3,5},... | collective-permute-start | bytes 405512 | tf_op jit(solution)/shard_map/ppermute | solution.py:156
  68.0 34.3 %collective-permute-start.12 = (bf16[66,8,128]{2,1,0:T(8,128)(2,1)S(1)}, bf16[66,8,128]{2,1,0:T(8,128)(2,1)S(1)}, u32[]{:S(2)}, u32[]{:S(2)}) collective-permute-start(bf16[66,8,128]{2,1,0:T(8,128)(2,1)S(1)} %get-tuple-element.17), channel_id=1, source_target_pairs={{0,12},{2,14},{4,0},{6,2},{8,4},{10,6},{12,8},{14,10},{1,13},{3,15... | collective-permute-start | bytes 405512 | tf_op jit(solution)/shard_map/ppermute | solution.py:156
  70.4 31.3 %collective-permute-start.11 = (bf16[66,8,128]{2,1,0:T(8,128)(2,1)S(1)}, bf16[66,8,128]{2,1,0:T(8,128)(2,1)S(1)}, u32[]{:S(2)}, u32[]{:S(2)}) collective-permute-start(bf16[66,8,128]{2,1,0:T(8,128)(2,1)S(1)} %get-tuple-element.18), channel_id=1, source_target_pairs={{0,4},{2,6},{4,8},{6,10},{8,12},{10,14},{12,0},{14,2},{1,5},{3,7},... | collective-permute-start | bytes 405512 | tf_op jit(solution)/shard_map/ppermute | solution.py:156
  71.0 20.4 %collective-permute-start.9 = (bf16[66,8,128]{2,1,0:T(8,128)(2,1)S(1)}, bf16[66,8,128]{2,1,0:T(8,128)(2,1)S(1)}, u32[]{:S(2)}, u32[]{:S(2)}) collective-permute-start(bf16[66,8,128]{2,1,0:T(8,128)(2,1)S(1)} %get-tuple-element.20), channel_id=1, source_target_pairs={{0,6},{2,8},{4,10},{6,12},{8,14},{10,0},{12,2},{14,4},{1,7},{3,9},... | collective-permute-start | bytes 405512 | tf_op jit(solution)/shard_map/ppermute | solution.py:156
  91.5 9.6 %collective-permute-start.10 = (bf16[66,8,128]{2,1,0:T(8,128)(2,1)S(1)}, bf16[66,8,128]{2,1,0:T(8,128)(2,1)S(1)}, u32[]{:S(2)}, u32[]{:S(2)}) collective-permute-start(bf16[66,8,128]{2,1,0:T(8,128)(2,1)S(1)} %get-tuple-element.19), channel_id=1, source_target_pairs={{0,10},{2,12},{4,14},{6,0},{8,2},{10,4},{12,6},{14,8},{1,11},{3,13... | collective-permute-start | bytes 405512 | tf_op jit(solution)/shard_map/ppermute | solution.py:156
  104.3 23.9 %collective-permute-start.15 = (bf16[33,8,8,128]{3,2,0,1:T(8,128)(2,1)}, bf16[33,8,8,128]{3,2,0,1:T(8,128)(2,1)S(1)}, u32[]{:S(2)}, u32[]{:S(2)}) collective-permute-start(bf16[33,8,8,128]{3,2,0,1:T(8,128)(2,1)} %get-tuple-element.38), channel_id=1, source_target_pairs={{0,1},{1,0},{2,3},{3,2},{4,5},{5,4},{6,7},{7,6},{8,9},{9,8},{10,11... | collective-permute-start | bytes 1622024 | tf_op jit(solution)/shard_map/ppermute | solution.py:139
  108.3 2.1 %collective-permute-start.16 = (bf16[8,16,8,128]{3,2,1,0:T(8,128)(2,1)S(1)}, bf16[8,16,8,128]{3,2,1,0:T(8,128)(2,1)S(1)}, u32[]{:S(2)}, u32[]{:S(2)}) collective-permute-start(bf16[8,16,8,128]{3,2,1,0:T(8,128)(2,1)S(1)} %all-to-all-done.1), channel_id=1, source_target_pairs={{0,1},{1,0},{2,3},{3,2},{4,5},{5,4},{6,7},{7,6},{8,9},{9,8},{10,11... | collective-permute-start | bytes 786440 | tf_op jit(solution)/shard_map/ppermute | solution.py:139
  142.1 1.6 %collective-permute-start.17 = (bf16[8,8,2048]{2,1,0:T(8,128)(2,1)S(1)}, bf16[8,8,2048]{2,1,0:T(8,128)(2,1)S(1)}, u32[]{:S(2)}, u32[]{:S(2)}) collective-permute-start(bf16[8,8,2048]{2,1,0:T(8,128)(2,1)S(1)} %fusion.7), channel_id=1, source_target_pairs={{0,1},{1,0},{2,3},{3,2},{4,5},{5,4},{6,7},{7,6},{8,9},{9,8},{10,11... | collective-permute-start | bytes 786440 | tf_op jit(solution)/shard_map/ppermute | solution.py:139
where the time goes:
time: 163 us; the launch traced here: 162 us
  starting transfers between devices  50 us (31%)
  waiting for transfers between devices  38.5 us (24%)
  Pallas kernels  38.2 us (23%)
  blocking collectives  16.1 us (10%)
  local copies, waits for them, and re-layouts  13 us (8%)
  other arithmetic  3.07 us (2%)
  matrix products  1.86 us (1%)
    ppermute x14, waiting for transfers between devices, send_over_z(): arrived.append(lax.ppermute(block, 'z', pairs))  35.2 us
    ppermute x14, starting transfers between devices, send_over_z(): arrived.append(lax.ppermute(block, 'z', pairs))  33.4 us
    pallas_call x1, Pallas kernels, make_image(): pl.pallas_call(functools.partial(image_kernel, 4), in_specs=[VMEM, VMEM],...  16.7 us
    all_to_all x1, blocking collectives, body(): parts = lax.all_to_all(parts, 'z', 0, 0, tiled=True)  16.1 us
    pallas_call x1, Pallas kernels, make_sigma(): pl.pallas_call(sigma_kernel, in_specs=[VMEM, VMEM], out_specs=VMEM, out_s...  11.4 us
    pallas_call x1, Pallas kernels, rotate(): pl.pallas_call(functools.partial(rotate_kernel, group, zs, rows), grid=(p...  10.2 us
    all_to_all x1, starting transfers between devices, body(): sources = lax.all_to_all(copies, SEC, 0, 0, tiled=True)  7.57 us
    ppermute x4, starting transfers between devices, other_core(): return lax.ppermute(x, 'core', [(0, 1), (1, 0)])  5.46 us
  transfers between devices with their start and end apart: 20, of which 9 were waited for; matrix products, arithmetic and copies ran while one was open for 7% of the time, Pallas kernels for 17%

commit v1 on v0

v1 whole, which is shorter than its diff:
```python
import functools

import jax
import jax.numpy as jnp
from jax import lax
from jax.experimental import pallas as pl
from jax.experimental.pallas import tpu as pltpu
from jax.sharding import Mesh
from jax.sharding import PartitionSpec as P


SEC = ("y", "x")
PAIR = ("z", "core")
FAR_FIRST = (4, 3, -3, 2, -2, 1, -1)
F32 = jnp.float32
BF16 = jnp.bfloat16
VMEM = pl.BlockSpec(memory_space=pltpu.VMEM)


def grant(mib):
    return pltpu.CompilerParams(vmem_limit_bytes=mib * 1024 * 1024)


def dot(a, b, dims):
    return lax.dot_general(a, b, (dims, ((), ())), preferred_element_type=F32)


def rotate_kernel(group, zs, rows, scalars, left, rotation, own, other, kept_ref, rows_ref):
    size, core = scalars[0], scalars[1]
    depth, width = rotation.shape

    @pl.when(pl.program_id(0) == 0)
    def _():
        live = lax.broadcasted_iota(jnp.int32, (depth, width), 1) < size
        kept = jnp.where(live, rotation[...].astype(F32), 0.0).astype(BF16)
        kept_ref[...] = kept
        slot = lax.broadcasted_iota(jnp.int32, (width, width), 0)
        target = lax.broadcasted_iota(jnp.int32, (width, width), 1)
        half = zs * rows
        which = (slot >= half).astype(jnp.int32)
        rest = slot - which * half
        place = core + which - 2 * core * which
        chip = lax.shift_right_logical(rest, 3)
        column = chip * (2 * rows) + place * rows + (rest - chip * rows)
        pick = jnp.where(column == target, 1.0, 0.0).astype(BF16)
        rows_ref[...] = dot(pick, kept, ((1,), (1,))).astype(BF16)

    kept = kept_ref[...]
    mine = rows_ref[...]
    parts = [dot(mine, left[g], ((1,), (0,))).astype(BF16) for g in range(group)]
    whole = dot(jnp.concatenate(parts, axis=0), kept, ((1,), (0,))).astype(BF16)
    for g in range(group):
        result = whole[g * width : (g + 1) * width].reshape(2, zs, rows, width)
        own[:, g] = result[0]
        other[:, g] = result[1]


def rotate(left, rotation, scalars, zs, rows, group):
    pairs, depth, _ = left.shape
    width = rotation.shape[1]
    shape = jax.ShapeDtypeStruct((zs, pairs, rows, width), BF16)
    block = pl.BlockSpec((zs, group, rows, width), lambda g: (0, g, 0, 0))
    return pl.pallas_call(
        functools.partial(rotate_kernel, group, zs, rows),
        grid=(pairs // group,),
        in_specs=[
            pl.BlockSpec(memory_space=pltpu.SMEM),
            pl.BlockSpec((group, depth, depth), lambda g: (g, 0, 0)),
            pl.BlockSpec((depth, width), lambda g: (0, 0)),
        ],
        out_specs=[block, block],
        out_shape=[shape, shape],
        scratch_shapes=[pltpu.VMEM((depth, width), BF16), pltpu.VMEM((width, depth), BF16)],
        compiler_params=grant(10),
    )(scalars, left, rotation)


def image_kernel(chunk, mixed, right, image):
    roots, width, _ = mixed.shape
    pairs = right.shape[0]

    def put(first, count):
        ops = right[pl.ds(first, count)].reshape(count * width, width)
        for start in range(0, roots, chunk):
            block = mixed[start : start + chunk].reshape(chunk * width, width)
            result = dot(block, ops, ((1,), (1,))).astype(BF16)
            for r in range(chunk):
                for j in range(count):
                    image[
                        pl.ds(pl.multiple_of((first + j) * width, width), width),
                        (start + r) * width : (start + r + 1) * width,
                    ] = result[r * width : (r + 1) * width, j * width : (j + 1) * width]

    def step(i, carry):
        put(4 * i, 2)
        put(4 * i + 2, 2)
        return carry

    lax.fori_loop(0, pairs // 4, step, 0)
    for first in range(pairs - pairs % 4, pairs):
        put(first, 1)


def make_image(mixed, right):
    roots, width, _ = mixed.shape
    pairs = right.shape[0]
    return pl.pallas_call(
        functools.partial(image_kernel, 4),
        in_specs=[VMEM, VMEM],
        out_specs=VMEM,
        out_shape=pltpu.VMEM((pairs * width, roots * width), BF16),
        compiler_params=grant(5),
    )(mixed, right)


def sigma_kernel(comp, image, own, other):
    pairs, width, _ = comp.shape
    half = own.shape[0]
    sums = jnp.zeros((width, image.shape[1]), F32)
    for q in range(0, pairs - 1, 2):
        two = jnp.concatenate([comp[q], comp[q + 1]], axis=1)
        sums += dot(two, image[q * width : (q + 2) * width], ((1,), (0,)))
    if pairs % 2:
        sums += dot(comp[pairs - 1], image[(pairs - 1) * width : pairs * width], ((1,), (0,)))
    own[...] = sums[:half]
    other[...] = sums[half:].astype(BF16)


def make_sigma(comp, image):
    half = comp.shape[1] // 2
    return pl.pallas_call(
        sigma_kernel,
        in_specs=[VMEM, VMEM],
        out_specs=[VMEM, VMEM],
        out_shape=[
            pltpu.VMEM((half, image.shape[1]), F32),
            pltpu.VMEM((half, image.shape[1]), BF16),
        ],
        compiler_params=grant(8),
    )(comp, image)


def join_kernel(shifts, zs, scalars, own, theirs, *blocks):
    pairs = own.shape[1]
    for shift, block in zip(shifts, blocks):
        chip = lax.rem(scalars[0] + shift + zs, zs)
        block[:pairs] = own[chip]
        block[pairs:] = theirs[chip]


def cut_kernel(shifts, zs, scalars, whole, *blocks):
    for shift, block in zip(shifts, blocks):
        block[...] = whole[lax.rem(scalars[0] + shift + zs, zs)]


def split_kernel(shifts, zs, scalars, *refs):
    blocks, (mine, theirs) = refs[:-2], refs[-2:]
    pairs = mine.shape[1]
    core = scalars[1]
    for shift, block in zip(shifts, blocks):
        chip = lax.rem(scalars[0] - shift + zs, zs)
        mine[chip] = block[pl.ds(core * pairs, pairs)]
        theirs[chip] = block[pl.ds((1 - core) * pairs, pairs)]


def gather_kernel(shifts, zs, scalars, *refs):
    blocks, whole = refs[:-1], refs[-1]
    for shift, block in zip(shifts, blocks):
        whole[lax.rem(scalars[0] - shift + zs, zs)] = block[...]


def move(kernel, scalars, arrays, shapes, mib):
    shifts = (0,) + FAR_FIRST
    return pl.pallas_call(
        functools.partial(kernel, shifts, lax.axis_size("z")),
        in_specs=[pl.BlockSpec(memory_space=pltpu.SMEM)] + [VMEM] * len(arrays),
        out_specs=[VMEM] * len(shapes),
        out_shape=[pltpu.VMEM(shape, BF16) for shape in shapes],
        compiler_params=grant(mib),
    )(scalars, *arrays)


def other_core(x):
    return lax.ppermute(x, "core", [(0, 1), (1, 0)])


def in_core_order(own, other, dim):
    first = lax.axis_index("core") == 0
    return jnp.where(
        first, jnp.stack([own, other], axis=dim), jnp.stack([other, own], axis=dim)
    )


def send_over_z(blocks):
    n = lax.axis_size("z")
    arrived = []
    for shift, block in zip(FAR_FIRST, blocks):
        pairs = [(i, (i + shift) % n) for i in range(n)]
        arrived.append(lax.ppermute(block, "z", pairs))
    return arrived


def body(left_ops, rotation, integrals, right_ops, states, sector_sizes, couplings, pair_order):
    core = lax.axis_index("core")
    zs = lax.axis_size("z")
    cores = lax.axis_size("core")
    me = lax.axis_index("z")
    width = rotation.shape[2]
    pairs = left_ops.shape[1]
    roots, rows = states.shape[1], states.shape[2]
    sectors = lax.axis_size(SEC)
    all_pairs = integrals.shape[1]

    def flip(x):
        parts = x.reshape(zs, cores, pairs, *x.shape[1:])
        return jnp.where(core == 0, parts, parts[:, ::-1]).reshape(x.shape)

    left = pltpu.with_memory_space_constraint(left_ops[0], pltpu.HBM)
    turn = pltpu.with_memory_space_constraint(rotation[0], pltpu.HBM)
    scalars = jnp.stack([sector_sizes[0], core.astype(jnp.int32)])
    own, other = rotate(left, turn, scalars, zs, rows, 11)
    theirs = other_core(other)

    copies = jnp.broadcast_to(states, (sectors, *states.shape[1:]))
    sources = lax.all_to_all(copies, SEC, 0, 0, tiled=True)

    place = jnp.stack([me, core]).astype(jnp.int32)
    message = (cores * pairs, rows, width)
    blocks = move(join_kernel, place, (own, theirs), [message] * zs, 4)
    arrived = send_over_z(blocks[1:])
    arrived = [pltpu.with_memory_space_constraint(block, pltpu.VMEM) for block in arrived]
    (rotated_all,) = move(gather_kernel, place, [blocks[0]] + arrived, [(zs, *message)], 4)
    rotated_all = rotated_all.reshape(all_pairs, rows, width)

    order = flip(pair_order)
    taken = (jnp.arange(all_pairs, dtype=jnp.int32)[:, None] == order[None, :]).astype(BF16)
    ordered = jnp.dot(integrals, taken, preferred_element_type=F32).astype(BF16)
    ordered, rotated_all = lax.optimization_barrier((ordered, rotated_all))

    sector_ids = jnp.arange(sectors, dtype=jnp.int32)
    weights = jnp.sum((couplings[0][:, None] == sector_ids[None, :]).astype(F32), axis=0)
    mixed_rows = jnp.sum(weights[:, None, None, None] * sources.astype(F32), axis=0).astype(BF16)
    copies = jnp.broadcast_to(mixed_rows[None], (zs, *mixed_rows.shape))
    mixed_z = lax.all_to_all(copies, "z", 0, 0, tiled=True)
    mixed_other = other_core(mixed_z)
    mixed = in_core_order(mixed_z, mixed_other, 1)
    mixed = mixed.transpose(2, 0, 1, 3, 4).reshape(roots, width, width)
    image = make_image(mixed, right_ops[0])

    comp = jnp.einsum("qi,iab->qab", ordered, rotated_all, preferred_element_type=F32)
    comp = comp.astype(BF16)
    comp = comp.reshape(zs, cores * pairs, rows, width)

    blocks = move(cut_kernel, place, (comp,), [message] * zs, 4)
    arrived = send_over_z(blocks[1:])
    arrived = [pltpu.with_memory_space_constraint(block, pltpu.VMEM) for block in arrived]
    half = (zs, pairs, rows, width)
    mine, theirs = move(split_kernel, place, [blocks[0]] + arrived, [half] * 2, 4)
    theirs = other_core(theirs)
    comp = jnp.stack([mine, theirs]).transpose(2, 0, 1, 3, 4)
    comp = comp.reshape(pairs, width, width)

    total, given = make_sigma(comp, image)
    theirs = other_core(given)
    parts = (total + theirs.astype(F32)).astype(BF16).reshape(zs, rows, roots * width)
    parts = lax.all_to_all(parts, "z", 0, 0, tiled=True)
    result = parts.astype(F32).sum(axis=0)
    return result.reshape(rows, roots, width).transpose(1, 0, 2)[None]


def solution(mesh):
    torus = Mesh(mesh.devices.reshape(4, 4, -1, 2), ("y", "x", "z", "core"))
    placed = (
        P(SEC, PAIR, None, None),
        P(SEC, None, None),
        P(),
        P(SEC, PAIR, None, None),
        P(SEC, None, PAIR, None),
        P(SEC),
        P(SEC, None),
        P(),
    )
    return jax.shard_map(
        body, mesh=torus, in_specs=placed, out_specs=P(SEC, None, PAIR, None), check_vma=False
    )
```

time: 163 us -> 114 us (0.70)
  Pallas kernels: 38.2 us -> 17.1 us
  waiting for transfers between devices: 38.5 us -> 25.8 us
  local copies, waits for them, and re-layouts: 13 us -> 3.05 us
  starting transfers between devices: 50 us -> 47 us
    ppermute x14, waiting for transfers between devices: 35.2 us -> 22.8 us  [send_over_z(): arrived.append(lax.ppermute(block, 'z', pairs))]
    pallas_call x1, Pallas kernels: 16.7 us -> 8.04 us  [make_image(): pl.pallas_call(functools.partial(image_kernel, 4), in_specs=[VMEM, VMEM],...]
    pallas_call x1 -> x5, Pallas kernels: 11.4 us -> 4.96 us  [the longest x4 2.49 us: move(): pl.pallas_call(functools.partial(kernel, shifts, lax.axis_size('z')), in_...]
    pallas_call x1, Pallas kernels: 10.2 us -> 4.12 us  [rotate(): pl.pallas_call(functools.partial(rotate_kernel, group, zs, rows), grid=(p...]
    ppermute x14, starting transfers between devices: 33.4 us -> 28.8 us  [send_over_z(): arrived.append(lax.ppermute(block, 'z', pairs))]
    unnamed x22 -> x12, local copies, waits for them, and re-layouts: 4.93 us -> 0.49 us
    all_to_all x1, starting transfers between devices: 3.55 us -> 6.79 us  [body(): mixed_z = lax.all_to_all(copies, 'z', 0, 0, tiled=True)]
    all_to_all x1, starting transfers between devices: 7.57 us -> 5.04 us  [body(): sources = lax.all_to_all(copies, SEC, 0, 0, tiled=True)]
  transfers between devices with their start and end apart: 20 -> 20, of which waited for: 9 -> 10; matrix products, arithmetic and copies ran while one was open for 7% -> 5% of each run, Pallas kernels for 17% -> 9%
where the time goes in v1:
time: 114 us
  starting transfers between devices  47 us (41%)
  waiting for transfers between devices  25.8 us (23%)
  Pallas kernels  17.1 us (15%)
  blocking collectives  14.7 us (13%)
  local copies, waits for them, and re-layouts  3.05 us (3%)
  matrix products  2.8 us (2%)
  other arithmetic  2.35 us (2%)
    ppermute x14, starting transfers between devices, send_over_z(): arrived.append(lax.ppermute(block, 'z', pairs))  28.8 us
    ppermute x14, waiting for transfers between devices, send_over_z(): arrived.append(lax.ppermute(block, 'z', pairs))  22.8 us
    all_to_all x1, blocking collectives, body(): parts = lax.all_to_all(parts, 'z', 0, 0, tiled=True)  14.7 us
    pallas_call x1, Pallas kernels, make_image(): pl.pallas_call(functools.partial(image_kernel, 4), in_specs=[VMEM, VMEM],...  8.04 us
    all_to_all x1, starting transfers between devices, body(): mixed_z = lax.all_to_all(copies, 'z', 0, 0, tiled=True)  6.79 us
    ppermute x4, starting transfers between devices, other_core(): return lax.ppermute(x, 'core', [(0, 1), (1, 0)])  6.3 us
    all_to_all x1, starting transfers between devices, body(): sources = lax.all_to_all(copies, SEC, 0, 0, tiled=True)  5.04 us
    pallas_call x1, Pallas kernels, rotate(): pl.pallas_call(functools.partial(rotate_kernel, group, zs, rows), grid=(p...  4.12 us
  transfers between devices with their start and end apart: 20, of which 10 were waited for; matrix products, arithmetic and copies ran while one was open for 5% of the time, Pallas kernels for 9%

profile of v1, /device:TPU:1, one launch (start us, length us, event | category | flops | bytes accessed | tf_op | source)
XLA Modules:
  0.0 113.7 jit_solution(8182344432443773579)
XLA Ops:
  0.8 4.1 %shard_map.82 = (bf16[8,33,8,128]{3,2,1,0:T(8,128)(2,1)S(1)}, bf16[8,33,8,128]{3,2,1,0:T(8,128)(2,1)S(1)}) custom-call(s32[2]{0:T(128)S(1)} %pad_add_fusion.1.scalars, bf16[33,256,256]{2,1,0:T(8,128)(2,1)} %bitcast.41, bf16[256,128]{1,0:T(8,128)(2,1)} %bitcast.45), custom_call_target="tpu_custom_call" | custom-call | tf_op jit(solution)/shard_map/pallas_call | solution.py:63
  4.9 3.3 %collective-permute-start = (bf16[8,33,8,128]{3,2,1,0:T(8,128)(2,1)S(1)}, bf16[8,33,8,128]{3,2,1,0:T(8,128)(2,1)S(1)}, u32[]{:S(2)}, u32[]{:S(2)}) collective-permute-start(bf16[8,33,8,128]{3,2,1,0:T(8,128)(2,1)S(1)} %get-tuple-element.30), channel_id=1, source_target_pairs={{0,1},{1,0},{2,3},{3,2},{4,5},{5,4},{6,7},{7,6},{8,9},{9,8},{10,11... | collective-permute-start | bytes 1622024 | tf_op jit(solution)/shard_map/ppermute | solution.py:184
  8.2 0.9 broadcast_in_dim.9
  9.1 5.0 %all-to-all-start = ((bf16[16,16,8,128]{3,2,1,0:T(8,128)(2,1)}), bf16[16,16,8,128]{3,2,1,0:T(8,128)(2,1)S(1)}, u32[]{:S(2)}, u32[]{:S(2)}) async-start(bf16[16,16,8,128]{3,2,1,0:T(8,128)(2,1)} %broadcast_in_dim.9), calls=%async_computation | async-start | bytes 1048576 | tf_op jit(solution)/shard_map/all_to_all | solution.py:225
  14.5 0.6 shard_map.83
  15.1 7.0 %collective-permute-start.1 = (bf16[66,8,128]{2,1,0:T(8,128)(2,1)S(1)}, bf16[66,8,128]{2,1,0:T(8,128)(2,1)S(1)}, u32[]{:S(2)}, u32[]{:S(2)}) collective-permute-start(bf16[66,8,128]{2,1,0:T(8,128)(2,1)S(1)} %get-tuple-element.32), channel_id=1, source_target_pairs={{0,8},{2,10},{4,12},{6,14},{8,0},{10,2},{12,4},{14,6},{1,9},{3,11}... | collective-permute-start | bytes 405512 | tf_op jit(solution)/shard_map/ppermute | solution.py:199
  22.1 1.6 %collective-permute-start.2 = (bf16[66,8,128]{2,1,0:T(8,128)(2,1)S(1)}, bf16[66,8,128]{2,1,0:T(8,128)(2,1)S(1)}, u32[]{:S(2)}, u32[]{:S(2)}) collective-permute-start(bf16[66,8,128]{2,1,0:T(8,128)(2,1)S(1)} %get-tuple-element.33), channel_id=1, source_target_pairs={{0,6},{2,8},{4,10},{6,12},{8,14},{10,0},{12,2},{14,4},{1,7},{3,9},... | collective-permute-start | bytes 405512 | tf_op jit(solution)/shard_map/ppermute | solution.py:199
  23.8 1.8 %fusion.1 = bf16[528,528]{0,1:T(8,128)(2,1)} fusion(bf16[528,528]{1,0:T(8,128)(2,1)S(1)} %copy-done, s32[528]{0:T(1024)S(1)} %eq.36), kind=kOutput, calls=%fused_computation.4 | convolution fusion | flops 295232256 | bytes 1117248 | tf_op jit(solution)/shard_map/dot_general | solution.py:237
  25.6 2.9 %collective-permute-start.3 = (bf16[66,8,128]{2,1,0:T(8,128)(2,1)S(1)}, bf16[66,8,128]{2,1,0:T(8,128)(2,1)S(1)}, u32[]{:S(2)}, u32[]{:S(2)}) collective-permute-start(bf16[66,8,128]{2,1,0:T(8,128)(2,1)S(1)} %get-tuple-element.34), channel_id=1, source_target_pairs={{0,10},{2,12},{4,14},{6,0},{8,2},{10,4},{12,6},{14,8},{1,11},{3,13... | collective-permute-start | bytes 405512 | tf_op jit(solution)/shard_map/ppermute | solution.py:199
  28.5 1.2 %collective-permute-start.4 = (bf16[66,8,128]{2,1,0:T(8,128)(2,1)S(1)}, bf16[66,8,128]{2,1,0:T(8,128)(2,1)S(1)}, u32[]{:S(2)}, u32[]{:S(2)}) collective-permute-start(bf16[66,8,128]{2,1,0:T(8,128)(2,1)S(1)} %get-tuple-element.35), channel_id=1, source_target_pairs={{0,4},{2,6},{4,8},{6,10},{8,12},{10,14},{12,0},{14,2},{1,5},{3,7},... | collective-permute-start | bytes 405512 | tf_op jit(solution)/shard_map/ppermute | solution.py:199
  29.7 2.4 %collective-permute-start.5 = (bf16[66,8,128]{2,1,0:T(8,128)(2,1)S(1)}, bf16[66,8,128]{2,1,0:T(8,128)(2,1)S(1)}, u32[]{:S(2)}, u32[]{:S(2)}) collective-permute-start(bf16[66,8,128]{2,1,0:T(8,128)(2,1)S(1)} %get-tuple-element.36), channel_id=1, source_target_pairs={{0,12},{2,14},{4,0},{6,2},{8,4},{10,6},{12,8},{14,10},{1,13},{3,15... | collective-permute-start | bytes 405512 | tf_op jit(solution)/shard_map/ppermute | solution.py:199
  32.1 0.7 collective-permute-start.6
  32.8 4.5 %collective-permute-done.2.refs_2_ = bf16[66,8,128]{2,1,0:T(8,128)(2,1)S(1)} collective-permute-done((bf16[66,8,128]{2,1,0:T(8,128)(2,1)S(1)}, bf16[66,8,128]{2,1,0:T(8,128)(2,1)S(1)}, u32[]{:S(2)}, u32[]{:S(2)}) %collective-permute-start.2) | collective-permute-done | bytes 135200 | tf_op jit(solution)/shard_map/ppermute | solution.py:199
  37.3 0.2 multiply_reduce_fusion
  37.4 0.7 broadcast_in_dim.10
  38.2 6.8 %all-to-all-start.1 = ((bf16[8,16,8,128]{3,2,1,0:T(8,128)(2,1)}), bf16[8,16,8,128]{3,2,1,0:T(8,128)(2,1)S(1)}, u32[]{:S(2)}, u32[]{:S(2)}) async-start(bf16[8,16,8,128]{3,2,1,0:T(8,128)(2,1)} %broadcast_in_dim.10), calls=%async_computation.1 | async-start | bytes 524288 | tf_op jit(solution)/shard_map/all_to_all | solution.py:244
  45.0 1.1 collective-permute-done.6.refs_6_
  46.1 1.2 %collective-permute-done.7.refs_7_ = bf16[66,8,128]{2,1,0:T(8,128)(2,1)S(1)} collective-permute-done((bf16[66,8,128]{2,1,0:T(8,128)(2,1)S(1)}, bf16[66,8,128]{2,1,0:T(8,128)(2,1)S(1)}, u32[]{:S(2)}, u32[]{:S(2)}) %collective-permute-start.7) | collective-permute-done | bytes 135200 | tf_op jit(solution)/shard_map/ppermute | solution.py:199
  47.3 0.6 shard_map.84
  47.9 0.5 copy-done.5
  48.4 1.0 convolution_convert_fusion
  49.4 0.3 copy.20
  49.7 0.6 shard_map.85
  50.3 3.2 %collective-permute-start.8 = (bf16[66,8,128]{2,1,0:T(8,128)(2,1)S(1)}, bf16[66,8,128]{2,1,0:T(8,128)(2,1)S(1)}, u32[]{:S(2)}, u32[]{:S(2)}) collective-permute-start(bf16[66,8,128]{2,1,0:T(8,128)(2,1)S(1)} %get-tuple-element.42), channel_id=1, source_target_pairs={{0,8},{2,10},{4,12},{6,14},{8,0},{10,2},{12,4},{14,6},{1,9},{3,11}... | collective-permute-start | bytes 405512 | tf_op jit(solution)/shard_map/ppermute | solution.py:199
  53.5 1.9 %collective-permute-start.9 = (bf16[66,8,128]{2,1,0:T(8,128)(2,1)S(1)}, bf16[66,8,128]{2,1,0:T(8,128)(2,1)S(1)}, u32[]{:S(2)}, u32[]{:S(2)}) collective-permute-start(bf16[66,8,128]{2,1,0:T(8,128)(2,1)S(1)} %get-tuple-element.43), channel_id=1, source_target_pairs={{0,6},{2,8},{4,10},{6,12},{8,14},{10,0},{12,2},{14,4},{1,7},{3,9},... | collective-permute-start | bytes 405512 | tf_op jit(solution)/shard_map/ppermute | solution.py:199
  55.4 2.6 %collective-permute-start.10 = (bf16[66,8,128]{2,1,0:T(8,128)(2,1)S(1)}, bf16[66,8,128]{2,1,0:T(8,128)(2,1)S(1)}, u32[]{:S(2)}, u32[]{:S(2)}) collective-permute-start(bf16[66,8,128]{2,1,0:T(8,128)(2,1)S(1)} %get-tuple-element.44), channel_id=1, source_target_pairs={{0,10},{2,12},{4,14},{6,0},{8,2},{10,4},{12,6},{14,8},{1,11},{3,13... | collective-permute-start | bytes 405512 | tf_op jit(solution)/shard_map/ppermute | solution.py:199
  58.0 0.3 collective-permute-start.11
  58.3 3.3 %collective-permute-start.12 = (bf16[66,8,128]{2,1,0:T(8,128)(2,1)S(1)}, bf16[66,8,128]{2,1,0:T(8,128)(2,1)S(1)}, u32[]{:S(2)}, u32[]{:S(2)}) collective-permute-start(bf16[66,8,128]{2,1,0:T(8,128)(2,1)S(1)} %get-tuple-element.46), channel_id=1, source_target_pairs={{0,12},{2,14},{4,0},{6,2},{8,4},{10,6},{12,8},{14,10},{1,13},{3,15... | collective-permute-start | bytes 405512 | tf_op jit(solution)/shard_map/ppermute | solution.py:199
  61.6 2.8 %collective-permute-done.8.refs_1_ = bf16[66,8,128]{2,1,0:T(8,128)(2,1)S(1)} collective-permute-done((bf16[66,8,128]{2,1,0:T(8,128)(2,1)S(1)}, bf16[66,8,128]{2,1,0:T(8,128)(2,1)S(1)}, u32[]{:S(2)}, u32[]{:S(2)}) %collective-permute-start.8) | collective-permute-done | bytes 135200 | tf_op jit(solution)/shard_map/ppermute | solution.py:199
  64.4 0.7 collective-permute-start.13
  65.1 4.1 %collective-permute-done.9.refs_2_ = bf16[66,8,128]{2,1,0:T(8,128)(2,1)S(1)} collective-permute-done((bf16[66,8,128]{2,1,0:T(8,128)(2,1)S(1)}, bf16[66,8,128]{2,1,0:T(8,128)(2,1)S(1)}, u32[]{:S(2)}, u32[]{:S(2)}) %collective-permute-start.9) | collective-permute-done | bytes 135200 | tf_op jit(solution)/shard_map/ppermute | solution.py:199
  69.1 1.1 collective-permute-start.14
  70.2 1.6 %collective-permute-done.11.refs_4_ = bf16[66,8,128]{2,1,0:T(8,128)(2,1)S(1)} collective-permute-done((bf16[66,8,128]{2,1,0:T(8,128)(2,1)S(1)}, bf16[66,8,128]{2,1,0:T(8,128)(2,1)S(1)}, u32[]{:S(2)}, u32[]{:S(2)}) %collective-permute-start.11) | collective-permute-done | bytes 135200 | tf_op jit(solution)/shard_map/ppermute | solution.py:199
  71.8 5.5 %collective-permute-done.12.refs_5_ = bf16[66,8,128]{2,1,0:T(8,128)(2,1)S(1)} collective-permute-done((bf16[66,8,128]{2,1,0:T(8,128)(2,1)S(1)}, bf16[66,8,128]{2,1,0:T(8,128)(2,1)S(1)}, u32[]{:S(2)}, u32[]{:S(2)}) %collective-permute-start.12) | collective-permute-done | bytes 135200 | tf_op jit(solution)/shard_map/ppermute | solution.py:199
  77.3 2.1 %collective-permute-done.13.refs_6_ = bf16[66,8,128]{2,1,0:T(8,128)(2,1)S(1)} collective-permute-done((bf16[66,8,128]{2,1,0:T(8,128)(2,1)S(1)}, bf16[66,8,128]{2,1,0:T(8,128)(2,1)S(1)}, u32[]{:S(2)}, u32[]{:S(2)}) %collective-permute-start.13) | collective-permute-done | bytes 135200 | tf_op jit(solution)/shard_map/ppermute | solution.py:199
  79.4 0.6 shard_map.86
  80.0 2.4 %collective-permute-start.15 = (bf16[8,33,8,128]{3,2,1,0:T(8,128)(2,1)S(1)}, bf16[8,33,8,128]{3,2,1,0:T(8,128)(2,1)}, u32[]{:S(2)}, u32[]{:S(2)}) collective-permute-start(bf16[8,33,8,128]{3,2,1,0:T(8,128)(2,1)S(1)} %get-tuple-element.50), channel_id=1, source_target_pairs={{0,1},{1,0},{2,3},{3,2},{4,5},{5,4},{6,7},{7,6},{8,9},{9,8},{10,11... | collective-permute-start | bytes 1622024 | tf_op jit(solution)/shard_map/ppermute | solution.py:184
  82.5 0.1 collective-permute-start.16
  82.6 1.8 %collective-permute-done.16 = bf16[8,16,8,128]{3,2,1,0:T(8,128)(2,1)S(1)} collective-permute-done((bf16[8,16,8,128]{3,2,1,0:T(8,128)(2,1)S(1)}, bf16[8,16,8,128]{3,2,1,0:T(8,128)(2,1)S(1)}, u32[]{:S(2)}, u32[]{:S(2)}) %collective-permute-start.16) | collective-permute-done | bytes 262176 | tf_op jit(solution)/shard_map/ppermute | solution.py:184
  84.5 0.1 copy.22
  84.6 8.0 %shard_map.87.image = bf16[4224,2048]{1,0:T(8,128)(2,1)S(1)} custom-call(bf16[16,128,128]{2,1,0:T(8,128)(2,1)S(1)} %bitcast.37, bf16[33,128,128]{2,1,0:T(8,128)(2,1)S(1)} %bitcast.38), custom_call_target="tpu_custom_call" | custom-call | tf_op jit(solution)/shard_map/pallas_call | solution.py:107
  92.7 1.1 %maximum_bitcast_fusion = bf16[33,2,8,8,128]{4,3,0,2,1:T(8,128)(2,1)S(1)} fusion(bf16[1,8,33,8,128]{4,3,2,1,0:T(8,128)(2,1)} %bitcast.9, bf16[1,8,33,8,128]{4,3,2,1,0:T(8,128)(2,1)S(1)} %bitcast.40), kind=kLoop, calls=%fused_computation.5 | loop fusion | flops 540672 | bytes 2162688 | tf_op jit(solution)/shard_map/transpose | solution.py:260
  93.9 0.3 copy.21
  94.2 2.5 %shard_map.88 = (f32[64,2048]{1,0:T(8,128)S(1)}, bf16[64,2048]{1,0:T(8,128)(2,1)S(1)}) custom-call(bf16[33,128,128]{2,1,0:T(8,128)(2,1)S(1)} %bitcast.35, bf16[4224,2048]{1,0:T(8,128)(2,1)S(1)} %shard_map.87.image), custom_call_target="tpu_custom_call" | custom-call | tf_op jit(solution)/shard_map/pallas_call | solution.py:131
  96.7 0.5 collective-permute-start.17
  97.1 1.2 %collective-permute-done.17 = bf16[64,2048]{1,0:T(8,128)(2,1)S(1)} collective-permute-done((bf16[64,2048]{1,0:T(8,128)(2,1)S(1)}, bf16[64,2048]{1,0:T(8,128)(2,1)S(1)}, u32[]{:S(2)}, u32[]{:S(2)}) %collective-permute-start.17) | collective-permute-done | bytes 262176 | tf_op jit(solution)/shard_map/ppermute | solution.py:184
  98.3 14.7 %all_to_all.15 = bf16[8,8,2048]{2,1,0:T(8,128)(2,1)S(1)} all-to-all(bf16[8,8,2048]{2,1,0:T(8,128)(2,1)S(1)} %fusion.7), channel_id=1, replica_groups=mesh['y'=4,'x'=4,'z'=8,'core'=2] {'z'}, dimensions={0} | all-to-all | bytes 524288 | tf_op jit(solution)/shard_map/all_to_all | solution.py:266
  113.1 0.7 convert_reduce_fusion
  (31 shorter events, 0.6 us)
Async XLA Ops:
  0.0 23.8 %copy-start = (bf16[528,528]{1,0:T(8,128)(2,1)S(1)}, bf16[528,528]{1,0:T(8,128)(2,1)}, u32[]{:S(2)}) copy-start(bf16[528,528]{1,0:T(8,128)(2,1)} %param.10) | copy-start | bytes 1672708
  0.8 7.4 %copy-start.2 = (bf16[1,16,8,128]{3,2,1,0:T(8,128)(2,1)S(1)}, bf16[1,16,8,128]{3,2,1,0:T(8,128)(2,1)}, u32[]{:S(2)}) copy-start(bf16[1,16,8,128]{3,2,1,0:T(8,128)(2,1)} %param.12) | copy-start | bytes 98308
  4.9 9.3 %copy-start.3 = (s32[528]{0:T(1024)S(1)}, s32[528]{0:T(1024)}, u32[]{:S(2)}) copy-start(s32[528]{0:T(1024)} %param.15) | copy-start | bytes 6340
  4.9 9.6 %collective-permute-start = (bf16[8,33,8,128]{3,2,1,0:T(8,128)(2,1)S(1)}, bf16[8,33,8,128]{3,2,1,0:T(8,128)(2,1)S(1)}, u32[]{:S(2)}, u32[]{:S(2)}) collective-permute-start(bf16[8,33,8,128]{3,2,1,0:T(8,128)(2,1)S(1)} %get-tuple-element.30), channel_id=1, source_target_pairs={{0,1},{1,0},{2,3},{3,2},{4,5},{5,4},{6,7},{7,6},{8,9},{9,8},{10,11... | collective-permute-start | bytes 1622024 | tf_op jit(solution)/shard_map/ppermute | solution.py:184
  9.1 28.1 %all-to-all-start = ((bf16[16,16,8,128]{3,2,1,0:T(8,128)(2,1)}), bf16[16,16,8,128]{3,2,1,0:T(8,128)(2,1)S(1)}, u32[]{:S(2)}, u32[]{:S(2)}) async-start(bf16[16,16,8,128]{3,2,1,0:T(8,128)(2,1)} %broadcast_in_dim.9), calls=%async_computation | async-start | bytes 1048576 | tf_op jit(solution)/shard_map/all_to_all | solution.py:225
  15.1 16.9 %collective-permute-start.1 = (bf16[66,8,128]{2,1,0:T(8,128)(2,1)S(1)}, bf16[66,8,128]{2,1,0:T(8,128)(2,1)S(1)}, u32[]{:S(2)}, u32[]{:S(2)}) collective-permute-start(bf16[66,8,128]{2,1,0:T(8,128)(2,1)S(1)} %get-tuple-element.32), channel_id=1, source_target_pairs={{0,8},{2,10},{4,12},{6,14},{8,0},{10,2},{12,4},{14,6},{1,9},{3,11}... | collective-permute-start | bytes 405512 | tf_op jit(solution)/shard_map/ppermute | solution.py:199
  22.1 3.4 %copy-start.4 = (s32[1,4]{1,0:T(1,128)S(1)}, s32[1,4]{1,0:T(1,128)}, u32[]{:S(2)}) copy-start(s32[1,4]{1,0:T(1,128)} %param.14) | copy-start | bytes 52
  22.1 15.1 %collective-permute-start.2 = (bf16[66,8,128]{2,1,0:T(8,128)(2,1)S(1)}, bf16[66,8,128]{2,1,0:T(8,128)(2,1)S(1)}, u32[]{:S(2)}, u32[]{:S(2)}) collective-permute-start(bf16[66,8,128]{2,1,0:T(8,128)(2,1)S(1)} %get-tuple-element.33), channel_id=1, source_target_pairs={{0,6},{2,8},{4,10},{6,12},{8,14},{10,0},{12,2},{14,4},{1,7},{3,9},... | collective-permute-start | bytes 405512 | tf_op jit(solution)/shard_map/ppermute | solution.py:199
  25.6 19.3 %collective-permute-start.3 = (bf16[66,8,128]{2,1,0:T(8,128)(2,1)S(1)}, bf16[66,8,128]{2,1,0:T(8,128)(2,1)S(1)}, u32[]{:S(2)}, u32[]{:S(2)}) collective-permute-start(bf16[66,8,128]{2,1,0:T(8,128)(2,1)S(1)} %get-tuple-element.34), channel_id=1, source_target_pairs={{0,10},{2,12},{4,14},{6,0},{8,2},{10,4},{12,6},{14,8},{1,11},{3,13... | collective-permute-start | bytes 405512 | tf_op jit(solution)/shard_map/ppermute | solution.py:199
  28.5 16.5 %collective-permute-start.4 = (bf16[66,8,128]{2,1,0:T(8,128)(2,1)S(1)}, bf16[66,8,128]{2,1,0:T(8,128)(2,1)S(1)}, u32[]{:S(2)}, u32[]{:S(2)}) collective-permute-start(bf16[66,8,128]{2,1,0:T(8,128)(2,1)S(1)} %get-tuple-element.35), channel_id=1, source_target_pairs={{0,4},{2,6},{4,8},{6,10},{8,12},{10,14},{12,0},{14,2},{1,5},{3,7},... | collective-permute-start | bytes 405512 | tf_op jit(solution)/shard_map/ppermute | solution.py:199
  29.7 15.3 %collective-permute-start.5 = (bf16[66,8,128]{2,1,0:T(8,128)(2,1)S(1)}, bf16[66,8,128]{2,1,0:T(8,128)(2,1)S(1)}, u32[]{:S(2)}, u32[]{:S(2)}) collective-permute-start(bf16[66,8,128]{2,1,0:T(8,128)(2,1)S(1)} %get-tuple-element.36), channel_id=1, source_target_pairs={{0,12},{2,14},{4,0},{6,2},{8,4},{10,6},{12,8},{14,10},{1,13},{3,15... | collective-permute-start | bytes 405512 | tf_op jit(solution)/shard_map/ppermute | solution.py:199
  32.1 14.0 %collective-permute-start.6 = (bf16[66,8,128]{2,1,0:T(8,128)(2,1)S(1)}, bf16[66,8,128]{2,1,0:T(8,128)(2,1)S(1)}, u32[]{:S(2)}, u32[]{:S(2)}) collective-permute-start(bf16[66,8,128]{2,1,0:T(8,128)(2,1)S(1)} %get-tuple-element.37), channel_id=1, source_target_pairs={{0,2},{2,4},{4,6},{6,8},{8,10},{10,12},{12,14},{14,0},{1,3},{3,5},... | collective-permute-start | bytes 405512 | tf_op jit(solution)/shard_map/ppermute | solution.py:199
  37.3 10.0 %collective-permute-start.7 = (bf16[66,8,128]{2,1,0:T(8,128)(2,1)S(1)}, bf16[66,8,128]{2,1,0:T(8,128)(2,1)S(1)}, u32[]{:S(2)}, u32[]{:S(2)}) collective-permute-start(bf16[66,8,128]{2,1,0:T(8,128)(2,1)S(1)} %get-tuple-element.38), channel_id=1, source_target_pairs={{0,14},{2,0},{4,2},{6,4},{8,6},{10,8},{12,10},{14,12},{1,15},{3,1}... | collective-permute-start | bytes 405512 | tf_op jit(solution)/shard_map/ppermute | solution.py:199
  38.2 44.3 %all-to-all-start.1 = ((bf16[8,16,8,128]{3,2,1,0:T(8,128)(2,1)}), bf16[8,16,8,128]{3,2,1,0:T(8,128)(2,1)S(1)}, u32[]{:S(2)}, u32[]{:S(2)}) async-start(bf16[8,16,8,128]{3,2,1,0:T(8,128)(2,1)} %broadcast_in_dim.10), calls=%async_computation.1 | async-start | bytes 524288 | tf_op jit(solution)/shard_map/all_to_all | solution.py:244
  47.3 1.1 copy-start.5
  50.3 14.1 %collective-permute-start.8 = (bf16[66,8,128]{2,1,0:T(8,128)(2,1)S(1)}, bf16[66,8,128]{2,1,0:T(8,128)(2,1)S(1)}, u32[]{:S(2)}, u32[]{:S(2)}) collective-permute-start(bf16[66,8,128]{2,1,0:T(8,128)(2,1)S(1)} %get-tuple-element.42), channel_id=1, source_target_pairs={{0,8},{2,10},{4,12},{6,14},{8,0},{10,2},{12,4},{14,6},{1,9},{3,11}... | collective-permute-start | bytes 405512 | tf_op jit(solution)/shard_map/ppermute | solution.py:199
  53.5 15.6 %collective-permute-start.9 = (bf16[66,8,128]{2,1,0:T(8,128)(2,1)S(1)}, bf16[66,8,128]{2,1,0:T(8,128)(2,1)S(1)}, u32[]{:S(2)}, u32[]{:S(2)}) collective-permute-start(bf16[66,8,128]{2,1,0:T(8,128)(2,1)S(1)} %get-tuple-element.43), channel_id=1, source_target_pairs={{0,6},{2,8},{4,10},{6,12},{8,14},{10,0},{12,2},{14,4},{1,7},{3,9},... | collective-permute-start | bytes 405512 | tf_op jit(solution)/shard_map/ppermute | solution.py:199
  55.4 14.8 %collective-permute-start.10 = (bf16[66,8,128]{2,1,0:T(8,128)(2,1)S(1)}, bf16[66,8,128]{2,1,0:T(8,128)(2,1)S(1)}, u32[]{:S(2)}, u32[]{:S(2)}) collective-permute-start(bf16[66,8,128]{2,1,0:T(8,128)(2,1)S(1)} %get-tuple-element.44), channel_id=1, source_target_pairs={{0,10},{2,12},{4,14},{6,0},{8,2},{10,4},{12,6},{14,8},{1,11},{3,13... | collective-permute-start | bytes 405512 | tf_op jit(solution)/shard_map/ppermute | solution.py:199
  58.0 13.8 %collective-permute-start.11 = (bf16[66,8,128]{2,1,0:T(8,128)(2,1)S(1)}, bf16[66,8,128]{2,1,0:T(8,128)(2,1)S(1)}, u32[]{:S(2)}, u32[]{:S(2)}) collective-permute-start(bf16[66,8,128]{2,1,0:T(8,128)(2,1)S(1)} %get-tuple-element.45), channel_id=1, source_target_pairs={{0,4},{2,6},{4,8},{6,10},{8,12},{10,14},{12,0},{14,2},{1,5},{3,7},... | collective-permute-start | bytes 405512 | tf_op jit(solution)/shard_map/ppermute | solution.py:199
  58.3 19.1 %collective-permute-start.12 = (bf16[66,8,128]{2,1,0:T(8,128)(2,1)S(1)}, bf16[66,8,128]{2,1,0:T(8,128)(2,1)S(1)}, u32[]{:S(2)}, u32[]{:S(2)}) collective-permute-start(bf16[66,8,128]{2,1,0:T(8,128)(2,1)S(1)} %get-tuple-element.46), channel_id=1, source_target_pairs={{0,12},{2,14},{4,0},{6,2},{8,4},{10,6},{12,8},{14,10},{1,13},{3,15... | collective-permute-start | bytes 405512 | tf_op jit(solution)/shard_map/ppermute | solution.py:199
  64.4 15.0 %collective-permute-start.13 = (bf16[66,8,128]{2,1,0:T(8,128)(2,1)S(1)}, bf16[66,8,128]{2,1,0:T(8,128)(2,1)S(1)}, u32[]{:S(2)}, u32[]{:S(2)}) collective-permute-start(bf16[66,8,128]{2,1,0:T(8,128)(2,1)S(1)} %get-tuple-element.47), channel_id=1, source_target_pairs={{0,2},{2,4},{4,6},{6,8},{8,10},{10,12},{12,14},{14,0},{1,3},{3,5},... | collective-permute-start | bytes 405512 | tf_op jit(solution)/shard_map/ppermute | solution.py:199
  69.1 10.3 %collective-permute-start.14 = (bf16[66,8,128]{2,1,0:T(8,128)(2,1)S(1)}, bf16[66,8,128]{2,1,0:T(8,128)(2,1)S(1)}, u32[]{:S(2)}, u32[]{:S(2)}) collective-permute-start(bf16[66,8,128]{2,1,0:T(8,128)(2,1)S(1)} %get-tuple-element.48), channel_id=1, source_target_pairs={{0,14},{2,0},{4,2},{6,4},{8,6},{10,8},{12,10},{14,12},{1,15},{3,1}... | collective-permute-start | bytes 405512 | tf_op jit(solution)/shard_map/ppermute | solution.py:199
  80.0 4.6 %copy-start.1 = (bf16[1,33,128,128]{3,2,1,0:T(8,128)(2,1)S(1)}, bf16[1,33,128,128]{3,2,1,0:T(8,128)(2,1)}, u32[]{:S(2)}) copy-start(bf16[1,33,128,128]{3,2,1,0:T(8,128)(2,1)} %param.11) | copy-start | bytes 3244036
  80.0 12.7 %collective-permute-start.15 = (bf16[8,33,8,128]{3,2,1,0:T(8,128)(2,1)S(1)}, bf16[8,33,8,128]{3,2,1,0:T(8,128)(2,1)}, u32[]{:S(2)}, u32[]{:S(2)}) collective-permute-start(bf16[8,33,8,128]{3,2,1,0:T(8,128)(2,1)S(1)} %get-tuple-element.50), channel_id=1, source_target_pairs={{0,1},{1,0},{2,3},{3,2},{4,5},{5,4},{6,7},{7,6},{8,9},{9,8},{10,11... | collective-permute-start | bytes 1622024 | tf_op jit(solution)/shard_map/ppermute | solution.py:184
  82.5 1.9 %collective-permute-start.16 = (bf16[8,16,8,128]{3,2,1,0:T(8,128)(2,1)S(1)}, bf16[8,16,8,128]{3,2,1,0:T(8,128)(2,1)S(1)}, u32[]{:S(2)}, u32[]{:S(2)}) collective-permute-start(bf16[8,16,8,128]{3,2,1,0:T(8,128)(2,1)S(1)} %all-to-all-done.1), channel_id=1, source_target_pairs={{0,1},{1,0},{2,3},{3,2},{4,5},{5,4},{6,7},{7,6},{8,9},{9,8},{10,11... | collective-permute-start | bytes 786440 | tf_op jit(solution)/shard_map/ppermute | solution.py:184
  96.7 1.6 %collective-permute-start.17 = (bf16[64,2048]{1,0:T(8,128)(2,1)S(1)}, bf16[64,2048]{1,0:T(8,128)(2,1)S(1)}, u32[]{:S(2)}, u32[]{:S(2)}) collective-permute-start(bf16[64,2048]{1,0:T(8,128)(2,1)S(1)} %get-tuple-element.52), channel_id=1, source_target_pairs={{0,1},{1,0},{2,3},{3,2},{4,5},{5,4},{6,7},{7,6},{8,9},{9,8},{10,11... | collective-permute-start | bytes 786440 | tf_op jit(solution)/shard_map/ppermute | solution.py:184

commit v2 on v1

--- a/solution.py
+++ b/solution.py
@@ -75,9 +75,15 @@
     )(scalars, left, rotation)
 
 
-def image_kernel(chunk, mixed, right, image):
-    roots, width, _ = mixed.shape
+def image_kernel(chunk, scalars, mine, theirs, right, image, placed, mixed):
+    zs, roots, _, width = mine.shape
     pairs = right.shape[0]
+    core = scalars[1]
+    for chip in range(zs):
+        placed[:, chip, core] = mine[chip]
+        placed[:, chip, 1 - core] = theirs[chip]
+    for root in range(roots):
+        mixed[root] = placed[root].reshape(width, width)
 
     def put(first, count):
         ops = right[pl.ds(first, count)].reshape(count * width, width)
@@ -101,21 +107,29 @@
         put(first, 1)
 
 
-def make_image(mixed, right):
-    roots, width, _ = mixed.shape
+def make_image(scalars, mine, theirs, right):
+    zs, roots, rows, width = mine.shape
     pairs = right.shape[0]
     return pl.pallas_call(
         functools.partial(image_kernel, 4),
-        in_specs=[VMEM, VMEM],
+        in_specs=[pl.BlockSpec(memory_space=pltpu.SMEM), VMEM, VMEM, VMEM],
         out_specs=VMEM,
         out_shape=pltpu.VMEM((pairs * width, roots * width), BF16),
-        compiler_params=grant(5),
-    )(mixed, right)
-
-
-def sigma_kernel(comp, image, own, other):
-    pairs, width, _ = comp.shape
+        scratch_shapes=[
+            pltpu.VMEM((roots, zs, width // (zs * rows), rows, width), BF16),
+            pltpu.VMEM((roots, width, width), BF16),
+        ],
+        compiler_params=grant(6),
+    )(scalars, mine, theirs, right)
+
+
+def sigma_kernel(mine, theirs, image, own, other):
+    pairs, width = mine.shape[1], mine.shape[3]
     half = own.shape[0]
+    comp = [
+        jnp.concatenate([part[:, q].reshape(half, width) for part in (mine, theirs)], axis=0)
+        for q in range(pairs)
+    ]
     sums = jnp.zeros((width, image.shape[1]), F32)
     for q in range(0, pairs - 1, 2):
         two = jnp.concatenate([comp[q], comp[q + 1]], axis=1)
@@ -126,31 +140,32 @@
     other[...] = sums[half:].astype(BF16)
 
 
-def make_sigma(comp, image):
-    half = comp.shape[1] // 2
+def make_sigma(mine, theirs, image):
+    half = mine.shape[0] * mine.shape[2]
     return pl.pallas_call(
         sigma_kernel,
-        in_specs=[VMEM, VMEM],
+        in_specs=[VMEM, VMEM, VMEM],
         out_specs=[VMEM, VMEM],
         out_shape=[
             pltpu.VMEM((half, image.shape[1]), F32),
             pltpu.VMEM((half, image.shape[1]), BF16),
         ],
         compiler_params=grant(8),
-    )(comp, image)
+    )(mine, theirs, image)
 
 
 def join_kernel(shifts, zs, scalars, own, theirs, *blocks):
     pairs = own.shape[1]
-    for shift, block in zip(shifts, blocks):
-        chip = lax.rem(scalars[0] + shift + zs, zs)
-        block[:pairs] = own[chip]
-        block[pairs:] = theirs[chip]
+    core = scalars[1]
+    for shift, block in zip(shifts, blocks):
+        chip = lax.rem(scalars[2] + shift + zs, zs)
+        block[pl.ds(core * pairs, pairs)] = own[chip]
+        block[pl.ds((1 - core) * pairs, pairs)] = theirs[chip]
 
 
 def cut_kernel(shifts, zs, scalars, whole, *blocks):
     for shift, block in zip(shifts, blocks):
-        block[...] = whole[lax.rem(scalars[0] + shift + zs, zs)]
+        block[...] = whole[lax.rem(scalars[2] + shift + zs, zs)]
 
 
 def split_kernel(shifts, zs, scalars, *refs):
@@ -158,7 +173,7 @@
     pairs = mine.shape[1]
     core = scalars[1]
     for shift, block in zip(shifts, blocks):
-        chip = lax.rem(scalars[0] - shift + zs, zs)
+        chip = lax.rem(scalars[2] - shift + zs, zs)
         mine[chip] = block[pl.ds(core * pairs, pairs)]
         theirs[chip] = block[pl.ds((1 - core) * pairs, pairs)]
 
@@ -166,7 +181,7 @@
 def gather_kernel(shifts, zs, scalars, *refs):
     blocks, whole = refs[:-1], refs[-1]
     for shift, block in zip(shifts, blocks):
-        whole[lax.rem(scalars[0] - shift + zs, zs)] = block[...]
+        whole[lax.rem(scalars[2] - shift + zs, zs)] = block[...]
 
 
 def move(kernel, scalars, arrays, shapes, mib):
@@ -182,13 +197,6 @@
 
 def other_core(x):
     return lax.ppermute(x, "core", [(0, 1), (1, 0)])
-
-
-def in_core_order(own, other, dim):
-    first = lax.axis_index("core") == 0
-    return jnp.where(
-        first, jnp.stack([own, other], axis=dim), jnp.stack([other, own], axis=dim)
-    )
 
 
 def send_over_z(blocks):
@@ -211,20 +219,15 @@
     sectors = lax.axis_size(SEC)
     all_pairs = integrals.shape[1]
 
-    def flip(x):
-        parts = x.reshape(zs, cores, pairs, *x.shape[1:])
-        return jnp.where(core == 0, parts, parts[:, ::-1]).reshape(x.shape)
-
     left = pltpu.with_memory_space_constraint(left_ops[0], pltpu.HBM)
     turn = pltpu.with_memory_space_constraint(rotation[0], pltpu.HBM)
-    scalars = jnp.stack([sector_sizes[0], core.astype(jnp.int32)])
-    own, other = rotate(left, turn, scalars, zs, rows, 11)
+    place = jnp.stack([sector_sizes[0], core.astype(jnp.int32), me.astype(jnp.int32)])
+    own, other = rotate(left, turn, place, zs, rows, 11)
     theirs = other_core(other)
 
     copies = jnp.broadcast_to(states, (sectors, *states.shape[1:]))
     sources = lax.all_to_all(copies, SEC, 0, 0, tiled=True)
 
-    place = jnp.stack([me, core]).astype(jnp.int32)
     message = (cores * pairs, rows, width)
     blocks = move(join_kernel, place, (own, theirs), [message] * zs, 4)
     arrived = send_over_z(blocks[1:])
@@ -232,8 +235,7 @@
     (rotated_all,) = move(gather_kernel, place, [blocks[0]] + arrived, [(zs, *message)], 4)
     rotated_all = rotated_all.reshape(all_pairs, rows, width)
 
-    order = flip(pair_order)
-    taken = (jnp.arange(all_pairs, dtype=jnp.int32)[:, None] == order[None, :]).astype(BF16)
+    taken = (jnp.arange(all_pairs, dtype=jnp.int32)[:, None] == pair_order[None, :]).astype(BF16)
     ordered = jnp.dot(integrals, taken, preferred_element_type=F32).astype(BF16)
     ordered, rotated_all = lax.optimization_barrier((ordered, rotated_all))
 
@@ -243,9 +245,7 @@
     copies = jnp.broadcast_to(mixed_rows[None], (zs, *mixed_rows.shape))
     mixed_z = lax.all_to_all(copies, "z", 0, 0, tiled=True)
     mixed_other = other_core(mixed_z)
-    mixed = in_core_order(mixed_z, mixed_other, 1)
-    mixed = mixed.transpose(2, 0, 1, 3, 4).reshape(roots, width, width)
-    image = make_image(mixed, right_ops[0])
+    image = make_image(place, mixed_z, mixed_other, right_ops[0])
 
     comp = jnp.einsum("qi,iab->qab", ordered, rotated_all, preferred_element_type=F32)
     comp = comp.astype(BF16)
@@ -257,10 +257,7 @@
     half = (zs, pairs, rows, width)
     mine, theirs = move(split_kernel, place, [blocks[0]] + arrived, [half] * 2, 4)
     theirs = other_core(theirs)
-    comp = jnp.stack([mine, theirs]).transpose(2, 0, 1, 3, 4)
-    comp = comp.reshape(pairs, width, width)
-
-    total, given = make_sigma(comp, image)
+    total, given = make_sigma(mine, theirs, image)
     theirs = other_core(given)
     parts = (total + theirs.astype(F32)).astype(BF16).reshape(zs, rows, roots * width)
     parts = lax.all_to_all(parts, "z", 0, 0, tiled=True)

time: 114 us -> 120 us (1.053)
  waiting for transfers between devices: 25.8 us -> 33 us
  starting transfers between devices: 47 us -> 44.7 us
  Pallas kernels: 17.1 us -> 18.8 us
  blocking collectives: 14.7 us -> 16.4 us
    ppermute x14, waiting for transfers between devices: 22.8 us -> 28.2 us  [send_over_z(): arrived.append(lax.ppermute(block, 'z', pairs))]
    all_to_all x1, starting transfers between devices: 6.79 us -> 3.41 us  [body(): mixed_z = lax.all_to_all(copies, 'z', 0, 0, tiled=True)]
    ppermute x4, waiting for transfers between devices: 2.99 us -> 4.86 us  [other_core(): return lax.ppermute(x, 'core', [(0, 1), (1, 0)])]
    all_to_all x1, starting transfers between devices: 5.04 us -> 6.81 us  [body(): sources = lax.all_to_all(copies, SEC, 0, 0, tiled=True)]
    all_to_all x1, blocking collectives: 14.7 us -> 16.4 us  [body(): parts = lax.all_to_all(parts, 'z', 0, 0, tiled=True)]
    ppermute x4, starting transfers between devices: 6.3 us -> 5.05 us  [other_core(): return lax.ppermute(x, 'core', [(0, 1), (1, 0)])]
    transpose x2 -> x0, other arithmetic: 1.23 us -> none  [the longest x1 1.15 us: body(): comp = jnp.stack([mine, theirs]).transpose(2, 0, 1, 3, 4)]
  transfers between devices with their start and end apart: 20 -> 20, of which waited for: 10 -> 11; matrix products, arithmetic and copies ran while one was open for 5% -> 4% of each run, Pallas kernels for 9% -> 10%
where the time goes in v2:
time: 120 us
  starting transfers between devices  44.7 us (37%)
  waiting for transfers between devices  33 us (28%)
  Pallas kernels  18.8 us (16%)
  blocking collectives  16.4 us (14%)
  other arithmetic  2.1 us (2%)
  local copies, waits for them, and re-layouts  1.94 us (2%)
  matrix products  1.93 us (2%)
    ppermute x14, starting transfers between devices, send_over_z(): arrived.append(lax.ppermute(block, 'z', pairs))  29.4 us
    ppermute x14, waiting for transfers between devices, send_over_z(): arrived.append(lax.ppermute(block, 'z', pairs))  28.2 us
    all_to_all x1, blocking collectives, body(): parts = lax.all_to_all(parts, 'z', 0, 0, tiled=True)  16.4 us
    pallas_call x1, Pallas kernels, make_image(): pl.pallas_call(functools.partial(image_kernel, 4), in_specs=[pl.BlockSpec...  8.8 us
    all_to_all x1, starting transfers between devices, body(): sources = lax.all_to_all(copies, SEC, 0, 0, tiled=True)  6.81 us
    ppermute x4, starting transfers between devices, other_core(): return lax.ppermute(x, 'core', [(0, 1), (1, 0)])  5.05 us
    ppermute x4, waiting for transfers between devices, other_core(): return lax.ppermute(x, 'core', [(0, 1), (1, 0)])  4.86 us
    pallas_call x1, Pallas kernels, rotate(): pl.pallas_call(functools.partial(rotate_kernel, group, zs, rows), grid=(p...  4.11 us
  transfers between devices with their start and end apart: 20, of which 11 were waited for; matrix products, arithmetic and copies ran while one was open for 4% of the time, Pallas kernels for 10%

profile of v2, /device:TPU:1, one launch (start us, length us, event | category | flops | bytes accessed | tf_op | source)
XLA Modules:
  0.0 119.7 jit_solution(2927794053389642362)
XLA Ops:
  0.7 0.1 pad_add_fusion.scalars
  0.8 4.1 %shard_map.82 = (bf16[8,33,8,128]{3,2,1,0:T(8,128)(2,1)S(1)}, bf16[8,33,8,128]{3,2,1,0:T(8,128)(2,1)S(1)}) custom-call(s32[3]{0:T(128)S(1)} %pad_add_fusion.scalars, bf16[33,256,256]{2,1,0:T(8,128)(2,1)} %bitcast.25, bf16[256,128]{1,0:T(8,128)(2,1)} %bitcast.26), custom_call_target="tpu_custom_call" | custom-call | tf_op jit(solution)/shard_map/pallas_call | solution.py:63
  4.9 0.0 copy-start.2
  4.9 3.3 %collective-permute-start = (bf16[8,33,8,128]{3,2,1,0:T(8,128)(2,1)S(1)}, bf16[8,33,8,128]{3,2,1,0:T(8,128)(2,1)S(1)}, u32[]{:S(2)}, u32[]{:S(2)}) collective-permute-start(bf16[8,33,8,128]{3,2,1,0:T(8,128)(2,1)S(1)} %get-tuple-element.30), channel_id=1, source_target_pairs={{0,1},{1,0},{2,3},{3,2},{4,5},{5,4},{6,7},{7,6},{8,9},{9,8},{10,11... | collective-permute-start | bytes 1622024 | tf_op jit(solution)/shard_map/ppermute | solution.py:199
  8.2 1.6 %collective-permute-done.theirs = bf16[8,33,8,128]{3,2,1,0:T(8,128)(2,1)S(1)} collective-permute-done((bf16[8,33,8,128]{3,2,1,0:T(8,128)(2,1)S(1)}, bf16[8,33,8,128]{3,2,1,0:T(8,128)(2,1)S(1)}, u32[]{:S(2)}, u32[]{:S(2)}) %collective-permute-start) | collective-permute-done | bytes 540704 | tf_op jit(solution)/shard_map/ppermute | solution.py:199
  9.8 0.6 shard_map.83
  10.4 5.3 %collective-permute-start.1 = (bf16[66,8,128]{2,1,0:T(8,128)(2,1)S(1)}, bf16[66,8,128]{2,1,0:T(8,128)(2,1)S(1)}, u32[]{:S(2)}, u32[]{:S(2)}) collective-permute-start(bf16[66,8,128]{2,1,0:T(8,128)(2,1)S(1)} %get-tuple-element.32), channel_id=1, source_target_pairs={{0,8},{2,10},{4,12},{6,14},{8,0},{10,2},{12,4},{14,6},{1,9},{3,11}... | collective-permute-start | bytes 405512 | tf_op jit(solution)/shard_map/ppermute | solution.py:207
  15.7 1.6 %collective-permute-start.2 = (bf16[66,8,128]{2,1,0:T(8,128)(2,1)S(1)}, bf16[66,8,128]{2,1,0:T(8,128)(2,1)S(1)}, u32[]{:S(2)}, u32[]{:S(2)}) collective-permute-start(bf16[66,8,128]{2,1,0:T(8,128)(2,1)S(1)} %get-tuple-element.33), channel_id=1, source_target_pairs={{0,6},{2,8},{4,10},{6,12},{8,14},{10,0},{12,2},{14,4},{1,7},{3,9},... | collective-permute-start | bytes 405512 | tf_op jit(solution)/shard_map/ppermute | solution.py:207
  17.3 0.9 broadcast_in_dim.9
  18.2 6.8 %all-to-all-start = ((bf16[16,16,8,128]{3,2,1,0:T(8,128)(2,1)}), bf16[16,16,8,128]{3,2,1,0:T(8,128)(2,1)}, u32[]{:S(2)}, u32[]{:S(2)}) async-start(bf16[16,16,8,128]{3,2,1,0:T(8,128)(2,1)} %broadcast_in_dim.9), calls=%async_computation | async-start | bytes 1048576 | tf_op jit(solution)/shard_map/all_to_all | solution.py:229
  25.1 2.9 %collective-permute-start.3 = (bf16[66,8,128]{2,1,0:T(8,128)(2,1)S(1)}, bf16[66,8,128]{2,1,0:T(8,128)(2,1)S(1)}, u32[]{:S(2)}, u32[]{:S(2)}) collective-permute-start(bf16[66,8,128]{2,1,0:T(8,128)(2,1)S(1)} %get-tuple-element.34), channel_id=1, source_target_pairs={{0,10},{2,12},{4,14},{6,0},{8,2},{10,4},{12,6},{14,8},{1,11},{3,13... | collective-permute-start | bytes 405512 | tf_op jit(solution)/shard_map/ppermute | solution.py:207
  28.0 1.2 collective-permute-start.4
  29.2 2.4 %collective-permute-start.5 = (bf16[66,8,128]{2,1,0:T(8,128)(2,1)S(1)}, bf16[66,8,128]{2,1,0:T(8,128)(2,1)S(1)}, u32[]{:S(2)}, u32[]{:S(2)}) collective-permute-start(bf16[66,8,128]{2,1,0:T(8,128)(2,1)S(1)} %get-tuple-element.36), channel_id=1, source_target_pairs={{0,12},{2,14},{4,0},{6,2},{8,4},{10,6},{12,8},{14,10},{1,13},{3,15... | collective-permute-start | bytes 405512 | tf_op jit(solution)/shard_map/ppermute | solution.py:207
  31.5 0.7 collective-permute-start.6
  32.3 1.9 %collective-permute-start.7 = (bf16[66,8,128]{2,1,0:T(8,128)(2,1)S(1)}, bf16[66,8,128]{2,1,0:T(8,128)(2,1)S(1)}, u32[]{:S(2)}, u32[]{:S(2)}) collective-permute-start(bf16[66,8,128]{2,1,0:T(8,128)(2,1)S(1)} %get-tuple-element.38), channel_id=1, source_target_pairs={{0,14},{2,0},{4,2},{6,4},{8,6},{10,8},{12,10},{14,12},{1,15},{3,1}... | collective-permute-start | bytes 405512 | tf_op jit(solution)/shard_map/ppermute | solution.py:207
  34.2 0.9 fusion.1
  35.1 0.1 convert_reduce_fusion.1
  35.2 2.5 %collective-permute-done.3.refs_3_ = bf16[66,8,128]{2,1,0:T(8,128)(2,1)S(1)} collective-permute-done((bf16[66,8,128]{2,1,0:T(8,128)(2,1)S(1)}, bf16[66,8,128]{2,1,0:T(8,128)(2,1)S(1)}, u32[]{:S(2)}, u32[]{:S(2)}) %collective-permute-start.3) | collective-permute-done | bytes 135200 | tf_op jit(solution)/shard_map/ppermute | solution.py:207
  37.7 5.6 %collective-permute-done.5.refs_5_ = bf16[66,8,128]{2,1,0:T(8,128)(2,1)S(1)} collective-permute-done((bf16[66,8,128]{2,1,0:T(8,128)(2,1)S(1)}, bf16[66,8,128]{2,1,0:T(8,128)(2,1)S(1)}, u32[]{:S(2)}, u32[]{:S(2)}) %collective-permute-start.5) | collective-permute-done | bytes 135200 | tf_op jit(solution)/shard_map/ppermute | solution.py:207
  43.3 3.4 %collective-permute-done.7.refs_7_ = bf16[66,8,128]{2,1,0:T(8,128)(2,1)S(1)} collective-permute-done((bf16[66,8,128]{2,1,0:T(8,128)(2,1)S(1)}, bf16[66,8,128]{2,1,0:T(8,128)(2,1)S(1)}, u32[]{:S(2)}, u32[]{:S(2)}) %collective-permute-start.7) | collective-permute-done | bytes 135200 | tf_op jit(solution)/shard_map/ppermute | solution.py:207
  46.7 0.6 shard_map.84
  47.4 1.0 convolution_convert_fusion
  48.4 0.3 copy.14
  48.7 0.6 shard_map.85
  49.3 0.6 collective-permute-start.8
  49.9 4.5 %collective-permute-start.9 = (bf16[66,8,128]{2,1,0:T(8,128)(2,1)S(1)}, bf16[66,8,128]{2,1,0:T(8,128)(2,1)S(1)}, u32[]{:S(2)}, u32[]{:S(2)}) collective-permute-start(bf16[66,8,128]{2,1,0:T(8,128)(2,1)S(1)} %get-tuple-element.43), channel_id=1, source_target_pairs={{0,6},{2,8},{4,10},{6,12},{8,14},{10,0},{12,2},{14,4},{1,7},{3,9},... | collective-permute-start | bytes 405512 | tf_op jit(solution)/shard_map/ppermute | solution.py:207
  54.4 1.2 %multiply_reduce_fusion = bf16[16,8,128]{2,1,0:T(8,128)(2,1)S(1)} fusion(bf16[16,16,8,128]{3,2,1,0:T(8,128)(2,1)} %all-to-all-done, f32[16]{0:T(128)S(1)} %convert_reduce_fusion.1), kind=kLoop, calls=%fused_computation.6 | loop fusion | flops 770048 | bytes 557120 | tf_op jit(solution)/shard_map/reduce_sum | solution.py:244
  55.6 0.7 broadcast_in_dim.10
  56.4 3.4 %all-to-all-start.1 = ((bf16[8,16,8,128]{3,2,1,0:T(8,128)(2,1)}), bf16[8,16,8,128]{3,2,1,0:T(8,128)(2,1)S(1)}, u32[]{:S(2)}, u32[]{:S(2)}) async-start(bf16[8,16,8,128]{3,2,1,0:T(8,128)(2,1)} %broadcast_in_dim.10), calls=%async_computation.1 | async-start | bytes 524288 | tf_op jit(solution)/shard_map/all_to_all | solution.py:246
  59.8 4.4 %collective-permute-start.10 = (bf16[66,8,128]{2,1,0:T(8,128)(2,1)S(1)}, bf16[66,8,128]{2,1,0:T(8,128)(2,1)S(1)}, u32[]{:S(2)}, u32[]{:S(2)}) collective-permute-start(bf16[66,8,128]{2,1,0:T(8,128)(2,1)S(1)} %get-tuple-element.44), channel_id=1, source_target_pairs={{0,10},{2,12},{4,14},{6,0},{8,2},{10,4},{12,6},{14,8},{1,11},{3,13... | collective-permute-start | bytes 405512 | tf_op jit(solution)/shard_map/ppermute | solution.py:207
  64.2 0.3 collective-permute-start.11
  64.5 3.3 %collective-permute-start.12 = (bf16[66,8,128]{2,1,0:T(8,128)(2,1)S(1)}, bf16[66,8,128]{2,1,0:T(8,128)(2,1)S(1)}, u32[]{:S(2)}, u32[]{:S(2)}) collective-permute-start(bf16[66,8,128]{2,1,0:T(8,128)(2,1)S(1)} %get-tuple-element.46), channel_id=1, source_target_pairs={{0,12},{2,14},{4,0},{6,2},{8,4},{10,6},{12,8},{14,10},{1,13},{3,15... | collective-permute-start | bytes 405512 | tf_op jit(solution)/shard_map/ppermute | solution.py:207
  67.8 0.3 collective-permute-start.13
  68.1 2.7 %collective-permute-done.9.refs_2_ = bf16[66,8,128]{2,1,0:T(8,128)(2,1)S(1)} collective-permute-done((bf16[66,8,128]{2,1,0:T(8,128)(2,1)S(1)}, bf16[66,8,128]{2,1,0:T(8,128)(2,1)S(1)}, u32[]{:S(2)}, u32[]{:S(2)}) %collective-permute-start.9) | collective-permute-done | bytes 135200 | tf_op jit(solution)/shard_map/ppermute | solution.py:207
  70.8 5.8 %collective-permute-done.11.refs_4_ = bf16[66,8,128]{2,1,0:T(8,128)(2,1)S(1)} collective-permute-done((bf16[66,8,128]{2,1,0:T(8,128)(2,1)S(1)}, bf16[66,8,128]{2,1,0:T(8,128)(2,1)S(1)}, u32[]{:S(2)}, u32[]{:S(2)}) %collective-permute-start.11) | collective-permute-done | bytes 135200 | tf_op jit(solution)/shard_map/ppermute | solution.py:207
  76.6 4.8 %collective-permute-done.12.refs_5_ = bf16[66,8,128]{2,1,0:T(8,128)(2,1)S(1)} collective-permute-done((bf16[66,8,128]{2,1,0:T(8,128)(2,1)S(1)}, bf16[66,8,128]{2,1,0:T(8,128)(2,1)S(1)}, u32[]{:S(2)}, u32[]{:S(2)}) %collective-permute-start.12) | collective-permute-done | bytes 135200 | tf_op jit(solution)/shard_map/ppermute | solution.py:207
  81.4 1.3 %collective-permute-done.13.refs_6_ = bf16[66,8,128]{2,1,0:T(8,128)(2,1)S(1)} collective-permute-done((bf16[66,8,128]{2,1,0:T(8,128)(2,1)S(1)}, bf16[66,8,128]{2,1,0:T(8,128)(2,1)S(1)}, u32[]{:S(2)}, u32[]{:S(2)}) %collective-permute-start.13) | collective-permute-done | bytes 135200 | tf_op jit(solution)/shard_map/ppermute | solution.py:207
  82.7 2.0 %collective-permute-done.14.refs_7_ = bf16[66,8,128]{2,1,0:T(8,128)(2,1)S(1)} collective-permute-done((bf16[66,8,128]{2,1,0:T(8,128)(2,1)S(1)}, bf16[66,8,128]{2,1,0:T(8,128)(2,1)S(1)}, u32[]{:S(2)}, u32[]{:S(2)}) %collective-permute-start.14) | collective-permute-done | bytes 135200 | tf_op jit(solution)/shard_map/ppermute | solution.py:207
  84.7 1.4 %shard_map.86 = (bf16[8,33,8,128]{3,2,1,0:T(8,128)(2,1)S(1)}, bf16[8,33,8,128]{3,2,1,0:T(8,128)(2,1)}) custom-call(s32[3]{0:T(128)S(1)} %pad_add_fusion.scalars, bf16[66,8,128]{2,1,0:T(8,128)(2,1)S(1)} %get-tuple-element.41.refs_0_, bf16[66,8,128]{2,1,0:T(8,128)(2,1)S(1)} %collective-permute-done.8.refs_1_, ...), custom_call_target="tpu_custom_call" | custom-call | tf_op jit(solution)/shard_map/pallas_call | solution.py:189
  86.1 1.3 %collective-permute-start.15 = (bf16[8,33,8,128]{3,2,1,0:T(8,128)(2,1)}, bf16[8,33,8,128]{3,2,1,0:T(8,128)(2,1)S(1)}, u32[]{:S(2)}, u32[]{:S(2)}) collective-permute-start(bf16[8,33,8,128]{3,2,1,0:T(8,128)(2,1)} %get-tuple-element.50), channel_id=1, source_target_pairs={{0,1},{1,0},{2,3},{3,2},{4,5},{5,4},{6,7},{7,6},{8,9},{9,8},{10,11... | collective-permute-start | bytes 1622024 | tf_op jit(solution)/shard_map/ppermute | solution.py:199
  87.4 2.1 %collective-permute-done.16.theirs = bf16[8,16,8,128]{3,2,1,0:T(8,128)(2,1)S(1)} collective-permute-done((bf16[8,16,8,128]{3,2,1,0:T(8,128)(2,1)S(1)}, bf16[8,16,8,128]{3,2,1,0:T(8,128)(2,1)S(1)}, u32[]{:S(2)}, u32[]{:S(2)}) %collective-permute-start.16) | collective-permute-done | bytes 262176 | tf_op jit(solution)/shard_map/ppermute | solution.py:199
  89.6 8.8 %shard_map.87.image = bf16[4224,2048]{1,0:T(8,128)(2,1)S(1)} custom-call(s32[3]{0:T(128)S(1)} %pad_add_fusion.scalars, bf16[8,16,8,128]{3,2,1,0:T(8,128)(2,1)S(1)} %all-to-all-done.1.mine, bf16[8,16,8,128]{3,2,1,0:T(8,128)(2,1)S(1)} %collective-permute-done.16.theirs, bf16[33,128,128]{2,1,0:T(8,128)(2,1)S(1)} %bitcast.24), custom_call_target="tpu_custom_call" | custom-call | tf_op jit(solution)/shard_map/pallas_call | solution.py:113
  98.4 2.6 %shard_map.88 = (f32[64,2048]{1,0:T(8,128)S(1)}, bf16[64,2048]{1,0:T(8,128)(2,1)S(1)}) custom-call(bf16[8,33,8,128]{3,2,1,0:T(8,128)(2,1)S(1)} %get-tuple-element.49.mine, bf16[8,33,8,128]{3,2,1,0:T(8,128)(2,1)S(1)} %collective-permute-done.15.theirs, bf16[4224,2048]{1,0:T(8,128)(2,1)S(1)} %shard_map.87.image), custom_call_target="tpu_custom_call" | custom-call | tf_op jit(solution)/shard_map/pallas_call | solution.py:145
  100.9 0.5 collective-permute-start.17
  101.4 1.2 collective-permute-done.17
  102.6 0.1 fusion.6
  102.6 16.4 %all_to_all.15 = bf16[8,8,2048]{2,1,0:T(8,128)(2,1)S(1)} all-to-all(bf16[8,8,2048]{2,1,0:T(8,128)(2,1)S(1)} %fusion.6), channel_id=1, replica_groups=mesh['y'=4,'x'=4,'z'=8,'core'=2] {'z'}, dimensions={0} | all-to-all | bytes 524288 | tf_op jit(solution)/shard_map/all_to_all | solution.py:263
  119.1 0.7 convert_reduce_fusion
  (20 shorter events, 0.0 us)
Async XLA Ops:
  0.0 34.2 %copy-start = (bf16[528,528]{1,0:T(8,128)(2,1)S(1)}, bf16[528,528]{1,0:T(8,128)(2,1)}, u32[]{:S(2)}) copy-start(bf16[528,528]{1,0:T(8,128)(2,1)} %param.10) | copy-start | bytes 1672708
  4.9 12.4 %copy-start.2 = (bf16[1,16,8,128]{3,2,1,0:T(8,128)(2,1)S(1)}, bf16[1,16,8,128]{3,2,1,0:T(8,128)(2,1)}, u32[]{:S(2)}) copy-start(bf16[1,16,8,128]{3,2,1,0:T(8,128)(2,1)} %param.12) | copy-start | bytes 98308
  4.9 4.8 %collective-permute-start = (bf16[8,33,8,128]{3,2,1,0:T(8,128)(2,1)S(1)}, bf16[8,33,8,128]{3,2,1,0:T(8,128)(2,1)S(1)}, u32[]{:S(2)}, u32[]{:S(2)}) collective-permute-start(bf16[8,33,8,128]{3,2,1,0:T(8,128)(2,1)S(1)} %get-tuple-element.30), channel_id=1, source_target_pairs={{0,1},{1,0},{2,3},{3,2},{4,5},{5,4},{6,7},{7,6},{8,9},{9,8},{10,11... | collective-permute-start | bytes 1622024 | tf_op jit(solution)/shard_map/ppermute | solution.py:199
  9.8 24.5 %copy-start.3 = (s32[528]{0:T(1024)S(1)}, s32[528]{0:T(1024)}, u32[]{:S(2)}) copy-start(s32[528]{0:T(1024)} %param.15) | copy-start | bytes 6340
  10.4 21.1 %collective-permute-start.1 = (bf16[66,8,128]{2,1,0:T(8,128)(2,1)S(1)}, bf16[66,8,128]{2,1,0:T(8,128)(2,1)S(1)}, u32[]{:S(2)}, u32[]{:S(2)}) collective-permute-start(bf16[66,8,128]{2,1,0:T(8,128)(2,1)S(1)} %get-tuple-element.32), channel_id=1, source_target_pairs={{0,8},{2,10},{4,12},{6,14},{8,0},{10,2},{12,4},{14,6},{1,9},{3,11}... | collective-permute-start | bytes 405512 | tf_op jit(solution)/shard_map/ppermute | solution.py:207
  15.7 16.6 %collective-permute-start.2 = (bf16[66,8,128]{2,1,0:T(8,128)(2,1)S(1)}, bf16[66,8,128]{2,1,0:T(8,128)(2,1)S(1)}, u32[]{:S(2)}, u32[]{:S(2)}) collective-permute-start(bf16[66,8,128]{2,1,0:T(8,128)(2,1)S(1)} %get-tuple-element.33), channel_id=1, source_target_pairs={{0,6},{2,8},{4,10},{6,12},{8,14},{10,0},{12,2},{14,4},{1,7},{3,9},... | collective-permute-start | bytes 405512 | tf_op jit(solution)/shard_map/ppermute | solution.py:207
  18.2 36.2 %all-to-all-start = ((bf16[16,16,8,128]{3,2,1,0:T(8,128)(2,1)}), bf16[16,16,8,128]{3,2,1,0:T(8,128)(2,1)}, u32[]{:S(2)}, u32[]{:S(2)}) async-start(bf16[16,16,8,128]{3,2,1,0:T(8,128)(2,1)} %broadcast_in_dim.9), calls=%async_computation | async-start | bytes 1048576 | tf_op jit(solution)/shard_map/all_to_all | solution.py:229
  25.1 12.7 %collective-permute-start.3 = (bf16[66,8,128]{2,1,0:T(8,128)(2,1)S(1)}, bf16[66,8,128]{2,1,0:T(8,128)(2,1)S(1)}, u32[]{:S(2)}, u32[]{:S(2)}) collective-permute-start(bf16[66,8,128]{2,1,0:T(8,128)(2,1)S(1)} %get-tuple-element.34), channel_id=1, source_target_pairs={{0,10},{2,12},{4,14},{6,0},{8,2},{10,4},{12,6},{14,8},{1,11},{3,13... | collective-permute-start | bytes 405512 | tf_op jit(solution)/shard_map/ppermute | solution.py:207
  28.0 9.8 %collective-permute-start.4 = (bf16[66,8,128]{2,1,0:T(8,128)(2,1)S(1)}, bf16[66,8,128]{2,1,0:T(8,128)(2,1)S(1)}, u32[]{:S(2)}, u32[]{:S(2)}) collective-permute-start(bf16[66,8,128]{2,1,0:T(8,128)(2,1)S(1)} %get-tuple-element.35), channel_id=1, source_target_pairs={{0,4},{2,6},{4,8},{6,10},{8,12},{10,14},{12,0},{14,2},{1,5},{3,7},... | collective-permute-start | bytes 405512 | tf_op jit(solution)/shard_map/ppermute | solution.py:207
  29.2 14.2 %collective-permute-start.5 = (bf16[66,8,128]{2,1,0:T(8,128)(2,1)S(1)}, bf16[66,8,128]{2,1,0:T(8,128)(2,1)S(1)}, u32[]{:S(2)}, u32[]{:S(2)}) collective-permute-start(bf16[66,8,128]{2,1,0:T(8,128)(2,1)S(1)} %get-tuple-element.36), channel_id=1, source_target_pairs={{0,12},{2,14},{4,0},{6,2},{8,4},{10,6},{12,8},{14,10},{1,13},{3,15... | collective-permute-start | bytes 405512 | tf_op jit(solution)/shard_map/ppermute | solution.py:207
  31.5 11.8 %collective-permute-start.6 = (bf16[66,8,128]{2,1,0:T(8,128)(2,1)S(1)}, bf16[66,8,128]{2,1,0:T(8,128)(2,1)S(1)}, u32[]{:S(2)}, u32[]{:S(2)}) collective-permute-start(bf16[66,8,128]{2,1,0:T(8,128)(2,1)S(1)} %get-tuple-element.37), channel_id=1, source_target_pairs={{0,2},{2,4},{4,6},{6,8},{8,10},{10,12},{12,14},{14,0},{1,3},{3,5},... | collective-permute-start | bytes 405512 | tf_op jit(solution)/shard_map/ppermute | solution.py:207
  32.3 2.9 %copy-start.4 = (s32[1,4]{1,0:T(1,128)S(1)}, s32[1,4]{1,0:T(1,128)}, u32[]{:S(2)}) copy-start(s32[1,4]{1,0:T(1,128)} %param.14) | copy-start | bytes 52
  32.3 14.5 %collective-permute-start.7 = (bf16[66,8,128]{2,1,0:T(8,128)(2,1)S(1)}, bf16[66,8,128]{2,1,0:T(8,128)(2,1)S(1)}, u32[]{:S(2)}, u32[]{:S(2)}) collective-permute-start(bf16[66,8,128]{2,1,0:T(8,128)(2,1)S(1)} %get-tuple-element.38), channel_id=1, source_target_pairs={{0,14},{2,0},{4,2},{6,4},{8,6},{10,8},{12,10},{14,12},{1,15},{3,1}... | collective-permute-start | bytes 405512 | tf_op jit(solution)/shard_map/ppermute | solution.py:207
  49.3 18.4 %collective-permute-start.8 = (bf16[66,8,128]{2,1,0:T(8,128)(2,1)S(1)}, bf16[66,8,128]{2,1,0:T(8,128)(2,1)S(1)}, u32[]{:S(2)}, u32[]{:S(2)}) collective-permute-start(bf16[66,8,128]{2,1,0:T(8,128)(2,1)S(1)} %get-tuple-element.42), channel_id=1, source_target_pairs={{0,8},{2,10},{4,12},{6,14},{8,0},{10,2},{12,4},{14,6},{1,9},{3,11}... | collective-permute-start | bytes 405512 | tf_op jit(solution)/shard_map/ppermute | solution.py:207
  49.9 20.8 %collective-permute-start.9 = (bf16[66,8,128]{2,1,0:T(8,128)(2,1)S(1)}, bf16[66,8,128]{2,1,0:T(8,128)(2,1)S(1)}, u32[]{:S(2)}, u32[]{:S(2)}) collective-permute-start(bf16[66,8,128]{2,1,0:T(8,128)(2,1)S(1)} %get-tuple-element.43), channel_id=1, source_target_pairs={{0,6},{2,8},{4,10},{6,12},{8,14},{10,0},{12,2},{14,4},{1,7},{3,9},... | collective-permute-start | bytes 405512 | tf_op jit(solution)/shard_map/ppermute | solution.py:207
  55.6 34.0 %copy-start.1 = (bf16[1,33,128,128]{3,2,1,0:T(8,128)(2,1)S(1)}, bf16[1,33,128,128]{3,2,1,0:T(8,128)(2,1)}, u32[]{:S(2)}) copy-start(bf16[1,33,128,128]{3,2,1,0:T(8,128)(2,1)} %param.11) | copy-start | bytes 3244036
  56.4 31.1 %all-to-all-start.1 = ((bf16[8,16,8,128]{3,2,1,0:T(8,128)(2,1)}), bf16[8,16,8,128]{3,2,1,0:T(8,128)(2,1)S(1)}, u32[]{:S(2)}, u32[]{:S(2)}) async-start(bf16[8,16,8,128]{3,2,1,0:T(8,128)(2,1)} %broadcast_in_dim.10), calls=%async_computation.1 | async-start | bytes 524288 | tf_op jit(solution)/shard_map/all_to_all | solution.py:246
  59.8 11.0 %collective-permute-start.10 = (bf16[66,8,128]{2,1,0:T(8,128)(2,1)S(1)}, bf16[66,8,128]{2,1,0:T(8,128)(2,1)S(1)}, u32[]{:S(2)}, u32[]{:S(2)}) collective-permute-start(bf16[66,8,128]{2,1,0:T(8,128)(2,1)S(1)} %get-tuple-element.44), channel_id=1, source_target_pairs={{0,10},{2,12},{4,14},{6,0},{8,2},{10,4},{12,6},{14,8},{1,11},{3,13... | collective-permute-start | bytes 405512 | tf_op jit(solution)/shard_map/ppermute | solution.py:207
  64.2 12.4 %collective-permute-start.11 = (bf16[66,8,128]{2,1,0:T(8,128)(2,1)S(1)}, bf16[66,8,128]{2,1,0:T(8,128)(2,1)S(1)}, u32[]{:S(2)}, u32[]{:S(2)}) collective-permute-start(bf16[66,8,128]{2,1,0:T(8,128)(2,1)S(1)} %get-tuple-element.45), channel_id=1, source_target_pairs={{0,4},{2,6},{4,8},{6,10},{8,12},{10,14},{12,0},{14,2},{1,5},{3,7},... | collective-permute-start | bytes 405512 | tf_op jit(solution)/shard_map/ppermute | solution.py:207
  64.5 16.9 %collective-permute-start.12 = (bf16[66,8,128]{2,1,0:T(8,128)(2,1)S(1)}, bf16[66,8,128]{2,1,0:T(8,128)(2,1)S(1)}, u32[]{:S(2)}, u32[]{:S(2)}) collective-permute-start(bf16[66,8,128]{2,1,0:T(8,128)(2,1)S(1)} %get-tuple-element.46), channel_id=1, source_target_pairs={{0,12},{2,14},{4,0},{6,2},{8,4},{10,6},{12,8},{14,10},{1,13},{3,15... | collective-permute-start | bytes 405512 | tf_op jit(solution)/shard_map/ppermute | solution.py:207
  67.8 15.0 %collective-permute-start.13 = (bf16[66,8,128]{2,1,0:T(8,128)(2,1)S(1)}, bf16[66,8,128]{2,1,0:T(8,128)(2,1)S(1)}, u32[]{:S(2)}, u32[]{:S(2)}) collective-permute-start(bf16[66,8,128]{2,1,0:T(8,128)(2,1)S(1)} %get-tuple-element.47), channel_id=1, source_target_pairs={{0,2},{2,4},{4,6},{6,8},{8,10},{10,12},{12,14},{14,0},{1,3},{3,5},... | collective-permute-start | bytes 405512 | tf_op jit(solution)/shard_map/ppermute | solution.py:207
  70.8 13.9 %collective-permute-start.14 = (bf16[66,8,128]{2,1,0:T(8,128)(2,1)S(1)}, bf16[66,8,128]{2,1,0:T(8,128)(2,1)S(1)}, u32[]{:S(2)}, u32[]{:S(2)}) collective-permute-start(bf16[66,8,128]{2,1,0:T(8,128)(2,1)S(1)} %get-tuple-element.48), channel_id=1, source_target_pairs={{0,14},{2,0},{4,2},{6,4},{8,6},{10,8},{12,10},{14,12},{1,15},{3,1}... | collective-permute-start | bytes 405512 | tf_op jit(solution)/shard_map/ppermute | solution.py:207
  86.1 12.2 %collective-permute-start.15 = (bf16[8,33,8,128]{3,2,1,0:T(8,128)(2,1)}, bf16[8,33,8,128]{3,2,1,0:T(8,128)(2,1)S(1)}, u32[]{:S(2)}, u32[]{:S(2)}) collective-permute-start(bf16[8,33,8,128]{3,2,1,0:T(8,128)(2,1)} %get-tuple-element.50), channel_id=1, source_target_pairs={{0,1},{1,0},{2,3},{3,2},{4,5},{5,4},{6,7},{7,6},{8,9},{9,8},{10,11... | collective-permute-start | bytes 1622024 | tf_op jit(solution)/shard_map/ppermute | solution.py:199
  87.4 2.1 %collective-permute-start.16 = (bf16[8,16,8,128]{3,2,1,0:T(8,128)(2,1)S(1)}, bf16[8,16,8,128]{3,2,1,0:T(8,128)(2,1)S(1)}, u32[]{:S(2)}, u32[]{:S(2)}) collective-permute-start(bf16[8,16,8,128]{3,2,1,0:T(8,128)(2,1)S(1)} %all-to-all-done.1.mine), channel_id=1, source_target_pairs={{0,1},{1,0},{2,3},{3,2},{4,5},{5,4},{6,7},{7,6},{8,9},{9,8},{10,11... | collective-permute-start | bytes 786440 | tf_op jit(solution)/shard_map/ppermute | solution.py:199
  100.9 1.6 %collective-permute-start.17 = (bf16[64,2048]{1,0:T(8,128)(2,1)S(1)}, bf16[64,2048]{1,0:T(8,128)(2,1)S(1)}, u32[]{:S(2)}, u32[]{:S(2)}) collective-permute-start(bf16[64,2048]{1,0:T(8,128)(2,1)S(1)} %get-tuple-element.52), channel_id=1, source_target_pairs={{0,1},{1,0},{2,3},{3,2},{4,5},{5,4},{6,7},{7,6},{8,9},{9,8},{10,11... | collective-permute-start | bytes 786440 | tf_op jit(solution)/shard_map/ppermute | solution.py:199

commit v3 on v2

--- a/solution.py
+++ b/solution.py
@@ -11,7 +11,7 @@
 
 SEC = ("y", "x")
 PAIR = ("z", "core")
-FAR_FIRST = (4, 3, -3, 2, -2, 1, -1)
+FAR_FIRST = (4, 3, -3, 2, -2, -1, 1)
 F32 = jnp.float32
 BF16 = jnp.bfloat16
 VMEM = pl.BlockSpec(memory_space=pltpu.VMEM)
@@ -25,54 +25,58 @@
     return lax.dot_general(a, b, (dims, ((), ())), preferred_element_type=F32)
 
 
-def rotate_kernel(group, zs, rows, scalars, left, rotation, own, other, kept_ref, rows_ref):
+def rotate_kernel(group, zs, rows, scalars, left_hbm, turn_hbm, own, other, left, turn, sems):
+    pairs, depth, _ = left.shape
+    width = turn.shape[1]
+    steps = pairs // group
+    first = pltpu.make_async_copy(turn_hbm, turn, sems.at[steps])
+    first.start()
+    copies = []
+    for step in range(steps):
+        span = pl.ds(step * group, group)
+        copies.append(pltpu.make_async_copy(left_hbm.at[span], left.at[span], sems.at[step]))
+        copies[-1].start()
     size, core = scalars[0], scalars[1]
-    depth, width = rotation.shape
-
-    @pl.when(pl.program_id(0) == 0)
-    def _():
-        live = lax.broadcasted_iota(jnp.int32, (depth, width), 1) < size
-        kept = jnp.where(live, rotation[...].astype(F32), 0.0).astype(BF16)
-        kept_ref[...] = kept
-        slot = lax.broadcasted_iota(jnp.int32, (width, width), 0)
-        target = lax.broadcasted_iota(jnp.int32, (width, width), 1)
-        half = zs * rows
-        which = (slot >= half).astype(jnp.int32)
-        rest = slot - which * half
-        place = core + which - 2 * core * which
-        chip = lax.shift_right_logical(rest, 3)
-        column = chip * (2 * rows) + place * rows + (rest - chip * rows)
-        pick = jnp.where(column == target, 1.0, 0.0).astype(BF16)
-        rows_ref[...] = dot(pick, kept, ((1,), (1,))).astype(BF16)
-
-    kept = kept_ref[...]
-    mine = rows_ref[...]
-    parts = [dot(mine, left[g], ((1,), (0,))).astype(BF16) for g in range(group)]
-    whole = dot(jnp.concatenate(parts, axis=0), kept, ((1,), (0,))).astype(BF16)
-    for g in range(group):
-        result = whole[g * width : (g + 1) * width].reshape(2, zs, rows, width)
-        own[:, g] = result[0]
-        other[:, g] = result[1]
-
-
-def rotate(left, rotation, scalars, zs, rows, group):
+    slot = lax.broadcasted_iota(jnp.int32, (width, width), 0)
+    target = lax.broadcasted_iota(jnp.int32, (width, width), 1)
+    which = (slot >= zs * rows).astype(jnp.int32)
+    rest = slot - which * (zs * rows)
+    spot = core + which - 2 * core * which
+    chip = lax.shift_right_logical(rest, 3)
+    column = chip * (2 * rows) + spot * rows + (rest - chip * rows)
+    pick = jnp.where(column == target, 1.0, 0.0).astype(BF16)
+    live = lax.broadcasted_iota(jnp.int32, (depth, width), 1) < size
+    first.wait()
+    kept = jnp.where(live, turn[...].astype(F32), 0.0).astype(BF16)
+    mine = dot(pick, kept, ((1,), (1,))).astype(BF16)
+    for step in range(steps):
+        copies[step].wait()
+        base = step * group
+        parts = [dot(mine, left[base + g], ((1,), (0,))).astype(BF16) for g in range(group)]
+        whole = dot(jnp.concatenate(parts, axis=0), kept, ((1,), (0,))).astype(BF16)
+        for g in range(group):
+            result = whole[g * width : (g + 1) * width].reshape(2, zs, rows, width)
+            own[:, base + g] = result[0]
+            other[:, base + g] = result[1]
+
+
+def rotate(left, turn, scalars, zs, rows, group):
     pairs, depth, _ = left.shape
-    width = rotation.shape[1]
-    shape = jax.ShapeDtypeStruct((zs, pairs, rows, width), BF16)
-    block = pl.BlockSpec((zs, group, rows, width), lambda g: (0, g, 0, 0))
+    width = turn.shape[1]
+    shape = pltpu.VMEM((zs, pairs, rows, width), BF16)
+    far = pl.BlockSpec(memory_space=pltpu.HBM)
     return pl.pallas_call(
         functools.partial(rotate_kernel, group, zs, rows),
-        grid=(pairs // group,),
-        in_specs=[
-            pl.BlockSpec(memory_space=pltpu.SMEM),
-            pl.BlockSpec((group, depth, depth), lambda g: (g, 0, 0)),
-            pl.BlockSpec((depth, width), lambda g: (0, 0)),
+        in_specs=[pl.BlockSpec(memory_space=pltpu.SMEM), far, far],
+        out_specs=[VMEM, VMEM],
+        out_shape=[shape, shape],
+        scratch_shapes=[
+            pltpu.VMEM((pairs, depth, depth), BF16),
+            pltpu.VMEM((depth, width), BF16),
+            pltpu.SemaphoreType.DMA((pairs // group + 1,)),
         ],
-        out_specs=[block, block],
-        out_shape=[shape, shape],
-        scratch_shapes=[pltpu.VMEM((depth, width), BF16), pltpu.VMEM((width, depth), BF16)],
-        compiler_params=grant(10),
-    )(scalars, left, rotation)
+        compiler_params=grant(12),
+    )(scalars, left, turn)
 
 
 def image_kernel(chunk, scalars, mine, theirs, right, image, placed, mixed):
@@ -123,35 +127,37 @@
     )(scalars, mine, theirs, right)
 
 
-def sigma_kernel(mine, theirs, image, own, other):
-    pairs, width = mine.shape[1], mine.shape[3]
-    half = own.shape[0]
-    comp = [
-        jnp.concatenate([part[:, q].reshape(half, width) for part in (mine, theirs)], axis=0)
-        for q in range(pairs)
-    ]
-    sums = jnp.zeros((width, image.shape[1]), F32)
+def sigma_kernel(shifts, scalars, mine_a, mine_b, theirs_a, theirs_b, image, own, other):
+    _, pairs, rows, width = mine_a.shape
+    zs = len(shifts)
+    comp = []
+    for q in range(pairs):
+        pieces = [part[:, q].reshape(-1, width) for part in (mine_a, mine_b, theirs_a, theirs_b)]
+        comp.append(jnp.concatenate(pieces, axis=0))
+    sums = jnp.zeros((2 * zs * rows, image.shape[1]), F32)
     for q in range(0, pairs - 1, 2):
         two = jnp.concatenate([comp[q], comp[q + 1]], axis=1)
         sums += dot(two, image[q * width : (q + 2) * width], ((1,), (0,)))
     if pairs % 2:
         sums += dot(comp[pairs - 1], image[(pairs - 1) * width : pairs * width], ((1,), (0,)))
-    own[...] = sums[:half]
-    other[...] = sums[half:].astype(BF16)
-
-
-def make_sigma(mine, theirs, image):
-    half = mine.shape[0] * mine.shape[2]
-    return pl.pallas_call(
-        sigma_kernel,
-        in_specs=[VMEM, VMEM, VMEM],
+    for slot, shift in enumerate(shifts):
+        chip = lax.rem(scalars[2] - shift + zs, zs)
+        own[chip] = sums[slot * rows : (slot + 1) * rows]
+        low = (zs + slot) * rows
+        other[chip] = sums[low : low + rows].astype(BF16)
+
+
+def make_sigma(scalars, parts, image):
+    rows = parts[0].shape[2]
+    shifts = (0,) + FAR_FIRST
+    shape = (len(shifts), rows, image.shape[1])
+    return pl.pallas_call(
+        functools.partial(sigma_kernel, shifts),
+        in_specs=[pl.BlockSpec(memory_space=pltpu.SMEM)] + [VMEM] * 5,
         out_specs=[VMEM, VMEM],
-        out_shape=[
-            pltpu.VMEM((half, image.shape[1]), F32),
-            pltpu.VMEM((half, image.shape[1]), BF16),
-        ],
+        out_shape=[pltpu.VMEM(shape, F32), pltpu.VMEM(shape, BF16)],
         compiler_params=grant(8),
-    )(mine, theirs, image)
+    )(scalars, *parts, image)
 
 
 def join_kernel(shifts, zs, scalars, own, theirs, *blocks):
@@ -172,10 +178,9 @@
     blocks, (mine, theirs) = refs[:-2], refs[-2:]
     pairs = mine.shape[1]
     core = scalars[1]
-    for shift, block in zip(shifts, blocks):
-        chip = lax.rem(scalars[2] - shift + zs, zs)
-        mine[chip] = block[pl.ds(core * pairs, pairs)]
-        theirs[chip] = block[pl.ds((1 - core) * pairs, pairs)]
+    for slot, block in enumerate(blocks):
+        mine[slot] = block[pl.ds(core * pairs, pairs)]
+        theirs[slot] = block[pl.ds((1 - core) * pairs, pairs)]
 
 
 def gather_kernel(shifts, zs, scalars, *refs):
@@ -254,12 +259,17 @@
     blocks = move(cut_kernel, place, (comp,), [message] * zs, 4)
     arrived = send_over_z(blocks[1:])
     arrived = [pltpu.with_memory_space_constraint(block, pltpu.VMEM) for block in arrived]
-    half = (zs, pairs, rows, width)
-    mine, theirs = move(split_kernel, place, [blocks[0]] + arrived, [half] * 2, 4)
-    theirs = other_core(theirs)
-    total, given = make_sigma(mine, theirs, image)
+    blocks = [blocks[0]] + arrived
+    shape = (zs - 2, pairs, rows, width)
+    mine_a, theirs_a = move(split_kernel, place, blocks[:-2], [shape] * 2, 4)
+    theirs_a = other_core(theirs_a)
+    shape = (2, pairs, rows, width)
+    mine_b, theirs_b = move(split_kernel, place, blocks[-2:], [shape] * 2, 4)
+    theirs_b = other_core(theirs_b)
+
+    total, given = make_sigma(place, (mine_a, mine_b, theirs_a, theirs_b), image)
     theirs = other_core(given)
-    parts = (total + theirs.astype(F32)).astype(BF16).reshape(zs, rows, roots * width)
+    parts = (total + theirs.astype(F32)).astype(BF16)
     parts = lax.all_to_all(parts, "z", 0, 0, tiled=True)
     result = parts.astype(F32).sum(axis=0)
     return result.reshape(rows, roots, width).transpose(1, 0, 2)[None]

time: 120 us -> 119 us (level)
  waiting for transfers between devices: 33 us -> 28 us
  starting transfers between devices: 44.7 us -> 46.9 us
    all_to_all x1, starting transfers between devices: 3.41 us -> 6.79 us  [body(): mixed_z = lax.all_to_all(copies, 'z', 0, 0, tiled=True)]
    ppermute x4 -> x5, waiting for transfers between devices: 4.86 us -> 1.5 us  [other_core(): return lax.ppermute(x, 'core', [(0, 1), (1, 0)])]
    ppermute x14, waiting for transfers between devices: 28.2 us -> 26.4 us  [send_over_z(): arrived.append(lax.ppermute(block, 'z', pairs))]
    all_to_all x1, starting transfers between devices: 6.81 us -> 5.23 us  [body(): sources = lax.all_to_all(copies, SEC, 0, 0, tiled=True)]
    ppermute x4 -> x5, starting transfers between devices: 5.05 us -> 6.16 us  [other_core(): return lax.ppermute(x, 'core', [(0, 1), (1, 0)])]
    pallas_call x4 -> x5, Pallas kernels: 3.3 us -> 3.73 us  [move(): pl.pallas_call(functools.partial(kernel, shifts, lax.axis_size('z')), in_...]
  transfers between devices with their start and end apart: 20 -> 21, of which waited for: 11 -> 9; matrix products, arithmetic and copies ran while one was open for 4% -> 5% of each run, Pallas kernels for 10% -> 10%
where the time goes in v3:
time: 119 us
  starting transfers between devices  46.9 us (39%)
  waiting for transfers between devices  28 us (24%)
  Pallas kernels  19.4 us (16%)
  blocking collectives  16.6 us (14%)
  matrix products  2.78 us (2%)
  local copies, waits for them, and re-layouts  2.39 us (2%)
  other arithmetic  2.08 us (2%)
    ppermute x14, starting transfers between devices, send_over_z(): arrived.append(lax.ppermute(block, 'z', pairs))  28.7 us
    ppermute x14, waiting for transfers between devices, send_over_z(): arrived.append(lax.ppermute(block, 'z', pairs))  26.4 us
    all_to_all x1, blocking collectives, body(): parts = lax.all_to_all(parts, 'z', 0, 0, tiled=True)  16.6 us
    pallas_call x1, Pallas kernels, make_image(): pl.pallas_call(functools.partial(image_kernel, 4), in_specs=[pl.BlockSpec...  8.73 us
    all_to_all x1, starting transfers between devices, body(): mixed_z = lax.all_to_all(copies, 'z', 0, 0, tiled=True)  6.79 us
    ppermute x5, starting transfers between devices, other_core(): return lax.ppermute(x, 'core', [(0, 1), (1, 0)])  6.16 us
    all_to_all x1, starting transfers between devices, body(): sources = lax.all_to_all(copies, SEC, 0, 0, tiled=True)  5.23 us
    pallas_call x1, Pallas kernels, rotate(): pl.pallas_call(functools.partial(rotate_kernel, group, zs, rows), in_spec...  3.83 us
  transfers between devices with their start and end apart: 21, of which 9 were waited for; matrix products, arithmetic and copies ran while one was open for 5% of the time, Pallas kernels for 10%

profile of v3, /device:TPU:1, one launch (start us, length us, event | category | flops | bytes accessed | tf_op | source)
XLA Modules:
  0.0 118.9 jit_solution(11715722153480920002)
XLA Ops:
  0.7 0.1 pad_add_fusion.scalars
  0.8 3.8 %shard_map.82 = (bf16[8,33,8,128]{3,2,1,0:T(8,128)(2,1)S(1)}, bf16[8,33,8,128]{3,2,1,0:T(8,128)(2,1)S(1)}) custom-call(s32[3]{0:T(128)S(1)} %pad_add_fusion.scalars, bf16[33,256,256]{2,1,0:T(8,128)(2,1)} %bitcast.23, bf16[256,128]{1,0:T(8,128)(2,1)} %bitcast.24), custom_call_target="tpu_custom_call" | custom-call | tf_op jit(solution)/shard_map/pallas_call | solution.py:68
  4.6 3.3 %collective-permute-start = (bf16[8,33,8,128]{3,2,1,0:T(8,128)(2,1)S(1)}, bf16[8,33,8,128]{3,2,1,0:T(8,128)(2,1)S(1)}, u32[]{:S(2)}, u32[]{:S(2)}) collective-permute-start(bf16[8,33,8,128]{3,2,1,0:T(8,128)(2,1)S(1)} %get-tuple-element.32), channel_id=1, source_target_pairs={{0,1},{1,0},{2,3},{3,2},{4,5},{5,4},{6,7},{7,6},{8,9},{9,8},{10,11... | collective-permute-start | bytes 1622024 | tf_op jit(solution)/shard_map/ppermute | solution.py:204
  7.9 0.9 broadcast_in_dim.9
  8.8 5.2 %all-to-all-start = ((bf16[16,16,8,128]{3,2,1,0:T(8,128)(2,1)}), bf16[16,16,8,128]{3,2,1,0:T(8,128)(2,1)}, u32[]{:S(2)}, u32[]{:S(2)}) async-start(bf16[16,16,8,128]{3,2,1,0:T(8,128)(2,1)} %broadcast_in_dim.9), calls=%async_computation | async-start | bytes 1048576 | tf_op jit(solution)/shard_map/all_to_all | solution.py:234
  14.1 0.6 shard_map.83
  14.7 7.0 %collective-permute-start.1 = (bf16[66,8,128]{2,1,0:T(8,128)(2,1)S(1)}, bf16[66,8,128]{2,1,0:T(8,128)(2,1)S(1)}, u32[]{:S(2)}, u32[]{:S(2)}) collective-permute-start(bf16[66,8,128]{2,1,0:T(8,128)(2,1)S(1)} %get-tuple-element.34), channel_id=1, source_target_pairs={{0,8},{2,10},{4,12},{6,14},{8,0},{10,2},{12,4},{14,6},{1,9},{3,11}... | collective-permute-start | bytes 405512 | tf_op jit(solution)/shard_map/ppermute | solution.py:212
  21.7 1.6 %collective-permute-start.2 = (bf16[66,8,128]{2,1,0:T(8,128)(2,1)S(1)}, bf16[66,8,128]{2,1,0:T(8,128)(2,1)S(1)}, u32[]{:S(2)}, u32[]{:S(2)}) collective-permute-start(bf16[66,8,128]{2,1,0:T(8,128)(2,1)S(1)} %get-tuple-element.35), channel_id=1, source_target_pairs={{0,6},{2,8},{4,10},{6,12},{8,14},{10,0},{12,2},{14,4},{1,7},{3,9},... | collective-permute-start | bytes 405512 | tf_op jit(solution)/shard_map/ppermute | solution.py:212
  23.4 1.8 %fusion.1 = bf16[528,528]{0,1:T(8,128)(2,1)} fusion(bf16[528,528]{1,0:T(8,128)(2,1)S(1)} %copy-done, s32[528]{0:T(1024)S(1)} %copy-done.3), kind=kOutput, calls=%fused_computation.4 | convolution fusion | flops 295232256 | bytes 1117248 | tf_op jit(solution)/shard_map/dot_general | solution.py:244
  25.1 0.1 convert_reduce_fusion.1
  25.2 2.8 %collective-permute-start.3 = (bf16[66,8,128]{2,1,0:T(8,128)(2,1)S(1)}, bf16[66,8,128]{2,1,0:T(8,128)(2,1)S(1)}, u32[]{:S(2)}, u32[]{:S(2)}) collective-permute-start(bf16[66,8,128]{2,1,0:T(8,128)(2,1)S(1)} %get-tuple-element.36), channel_id=1, source_target_pairs={{0,10},{2,12},{4,14},{6,0},{8,2},{10,4},{12,6},{14,8},{1,11},{3,13... | collective-permute-start | bytes 405512 | tf_op jit(solution)/shard_map/ppermute | solution.py:212
  28.0 1.2 %collective-permute-start.4 = (bf16[66,8,128]{2,1,0:T(8,128)(2,1)S(1)}, bf16[66,8,128]{2,1,0:T(8,128)(2,1)S(1)}, u32[]{:S(2)}, u32[]{:S(2)}) collective-permute-start(bf16[66,8,128]{2,1,0:T(8,128)(2,1)S(1)} %get-tuple-element.37), channel_id=1, source_target_pairs={{0,4},{2,6},{4,8},{6,10},{8,12},{10,14},{12,0},{14,2},{1,5},{3,7},... | collective-permute-start | bytes 405512 | tf_op jit(solution)/shard_map/ppermute | solution.py:212
  29.2 2.4 %collective-permute-start.5 = (bf16[66,8,128]{2,1,0:T(8,128)(2,1)S(1)}, bf16[66,8,128]{2,1,0:T(8,128)(2,1)S(1)}, u32[]{:S(2)}, u32[]{:S(2)}) collective-permute-start(bf16[66,8,128]{2,1,0:T(8,128)(2,1)S(1)} %get-tuple-element.38), channel_id=1, source_target_pairs={{0,12},{2,14},{4,0},{6,2},{8,4},{10,6},{12,8},{14,10},{1,13},{3,15... | collective-permute-start | bytes 405512 | tf_op jit(solution)/shard_map/ppermute | solution.py:212
  31.6 5.2 %collective-permute-done.2.refs_2_ = bf16[66,8,128]{2,1,0:T(8,128)(2,1)S(1)} collective-permute-done((bf16[66,8,128]{2,1,0:T(8,128)(2,1)S(1)}, bf16[66,8,128]{2,1,0:T(8,128)(2,1)S(1)}, u32[]{:S(2)}, u32[]{:S(2)}) %collective-permute-start.2) | collective-permute-done | bytes 135200 | tf_op jit(solution)/shard_map/ppermute | solution.py:212
  36.8 1.2 %multiply_reduce_fusion = bf16[16,8,128]{2,1,0:T(8,128)(2,1)S(1)} fusion(bf16[16,16,8,128]{3,2,1,0:T(8,128)(2,1)} %all-to-all-done, f32[16]{0:T(128)S(1)} %convert_reduce_fusion.1), kind=kLoop, calls=%fused_computation.6 | loop fusion | flops 770048 | bytes 557120 | tf_op jit(solution)/shard_map/reduce_sum | solution.py:249
  38.0 0.7 broadcast_in_dim.10
  38.8 6.8 %all-to-all-start.1 = ((bf16[8,16,8,128]{3,2,1,0:T(8,128)(2,1)}), bf16[8,16,8,128]{3,2,1,0:T(8,128)(2,1)S(1)}, u32[]{:S(2)}, u32[]{:S(2)}) async-start(bf16[8,16,8,128]{3,2,1,0:T(8,128)(2,1)} %broadcast_in_dim.10), calls=%async_computation.1 | async-start | bytes 524288 | tf_op jit(solution)/shard_map/all_to_all | solution.py:251
  45.6 1.2 %collective-permute-done.6.refs_6_ = bf16[66,8,128]{2,1,0:T(8,128)(2,1)S(1)} collective-permute-done((bf16[66,8,128]{2,1,0:T(8,128)(2,1)S(1)}, bf16[66,8,128]{2,1,0:T(8,128)(2,1)S(1)}, u32[]{:S(2)}, u32[]{:S(2)}) %collective-permute-start.6) | collective-permute-done | bytes 135200 | tf_op jit(solution)/shard_map/ppermute | solution.py:212
  46.8 0.6 shard_map.84
  47.5 0.5 copy-done.5
  47.9 1.0 convolution_convert_fusion
  49.0 0.3 copy.14
  49.3 1.3 %shard_map.85 = (bf16[66,8,128]{2,1,0:T(8,128)(2,1)S(1)}, bf16[66,8,128]{2,1,0:T(8,128)(2,1)S(1)}, bf16[66,8,128]{2,1,0:T(8,128)(2,1)S(1)}, bf16[66,8,128]{2,1,0...) custom-call(s32[3]{0:T(128)S(1)} %pad_add_fusion.scalars, ...), custom_call_target="tpu_custom_call" | custom-call | tf_op jit(solution)/shard_map/pallas_call | solution.py:194
  50.6 4.2 %collective-permute-start.8 = (bf16[66,8,128]{2,1,0:T(8,128)(2,1)S(1)}, bf16[66,8,128]{2,1,0:T(8,128)(2,1)S(1)}, u32[]{:S(2)}, u32[]{:S(2)}) collective-permute-start(bf16[66,8,128]{2,1,0:T(8,128)(2,1)S(1)} %get-tuple-element.44), channel_id=1, source_target_pairs={{0,8},{2,10},{4,12},{6,14},{8,0},{10,2},{12,4},{14,6},{1,9},{3,11}... | collective-permute-start | bytes 405512 | tf_op jit(solution)/shard_map/ppermute | solution.py:212
  54.7 0.8 collective-permute-start.9
  55.6 3.6 %collective-permute-start.10 = (bf16[66,8,128]{2,1,0:T(8,128)(2,1)S(1)}, bf16[66,8,128]{2,1,0:T(8,128)(2,1)S(1)}, u32[]{:S(2)}, u32[]{:S(2)}) collective-permute-start(bf16[66,8,128]{2,1,0:T(8,128)(2,1)S(1)} %get-tuple-element.46), channel_id=1, source_target_pairs={{0,10},{2,12},{4,14},{6,0},{8,2},{10,4},{12,6},{14,8},{1,11},{3,13... | collective-permute-start | bytes 405512 | tf_op jit(solution)/shard_map/ppermute | solution.py:212
  59.2 0.3 collective-permute-start.11
  59.5 3.3 %collective-permute-start.12 = (bf16[66,8,128]{2,1,0:T(8,128)(2,1)S(1)}, bf16[66,8,128]{2,1,0:T(8,128)(2,1)S(1)}, u32[]{:S(2)}, u32[]{:S(2)}) collective-permute-start(bf16[66,8,128]{2,1,0:T(8,128)(2,1)S(1)} %get-tuple-element.48), channel_id=1, source_target_pairs={{0,12},{2,14},{4,0},{6,2},{8,4},{10,6},{12,8},{14,10},{1,13},{3,15... | collective-permute-start | bytes 405512 | tf_op jit(solution)/shard_map/ppermute | solution.py:212
  62.8 1.4 %collective-permute-done.8.refs_1_ = bf16[66,8,128]{2,1,0:T(8,128)(2,1)S(1)} collective-permute-done((bf16[66,8,128]{2,1,0:T(8,128)(2,1)S(1)}, bf16[66,8,128]{2,1,0:T(8,128)(2,1)S(1)}, u32[]{:S(2)}, u32[]{:S(2)}) %collective-permute-start.8) | collective-permute-done | bytes 135200 | tf_op jit(solution)/shard_map/ppermute | solution.py:212
  64.1 0.0 collective-permute-done.9.refs_2_
  64.2 5.9 %collective-permute-done.10.refs_3_ = bf16[66,8,128]{2,1,0:T(8,128)(2,1)S(1)} collective-permute-done((bf16[66,8,128]{2,1,0:T(8,128)(2,1)S(1)}, bf16[66,8,128]{2,1,0:T(8,128)(2,1)S(1)}, u32[]{:S(2)}, u32[]{:S(2)}) %collective-permute-start.10) | collective-permute-done | bytes 135200 | tf_op jit(solution)/shard_map/ppermute | solution.py:212
  70.1 2.4 %collective-permute-done.11.refs_4_ = bf16[66,8,128]{2,1,0:T(8,128)(2,1)S(1)} collective-permute-done((bf16[66,8,128]{2,1,0:T(8,128)(2,1)S(1)}, bf16[66,8,128]{2,1,0:T(8,128)(2,1)S(1)}, u32[]{:S(2)}, u32[]{:S(2)}) %collective-permute-start.11) | collective-permute-done | bytes 135200 | tf_op jit(solution)/shard_map/ppermute | solution.py:212
  72.4 5.3 %collective-permute-done.12.refs_5_ = bf16[66,8,128]{2,1,0:T(8,128)(2,1)S(1)} collective-permute-done((bf16[66,8,128]{2,1,0:T(8,128)(2,1)S(1)}, bf16[66,8,128]{2,1,0:T(8,128)(2,1)S(1)}, u32[]{:S(2)}, u32[]{:S(2)}) %collective-permute-start.12) | collective-permute-done | bytes 135200 | tf_op jit(solution)/shard_map/ppermute | solution.py:212
  77.7 0.6 shard_map.86
  78.3 0.8 collective-permute-start.15
  79.1 1.0 collective-permute-start.13
  80.1 0.5 collective-permute-start.14
  80.6 0.7 collective-permute-start.17
  81.2 3.1 %collective-permute-done.13.refs_0_ = bf16[66,8,128]{2,1,0:T(8,128)(2,1)S(1)} collective-permute-done((bf16[66,8,128]{2,1,0:T(8,128)(2,1)}, bf16[66,8,128]{2,1,0:T(8,128)(2,1)S(1)}, u32[]{:S(2)}, u32[]{:S(2)}) %collective-permute-start.13) | collective-permute-done | bytes 135200 | tf_op jit(solution)/shard_map/ppermute | solution.py:212
  84.4 1.9 %collective-permute-done.14.refs_1_ = bf16[66,8,128]{2,1,0:T(8,128)(2,1)S(1)} collective-permute-done((bf16[66,8,128]{2,1,0:T(8,128)(2,1)}, bf16[66,8,128]{2,1,0:T(8,128)(2,1)S(1)}, u32[]{:S(2)}, u32[]{:S(2)}) %collective-permute-start.14) | collective-permute-done | bytes 135200 | tf_op jit(solution)/shard_map/ppermute | solution.py:212
  86.3 0.6 shard_map.87
  86.9 1.3 %collective-permute-start.16 = (bf16[2,33,8,128]{3,2,1,0:T(8,128)(2,1)S(1)}, bf16[2,33,8,128]{3,2,1,0:T(8,128)(2,1)S(1)}, u32[]{:S(2)}, u32[]{:S(2)}) collective-permute-start(bf16[2,33,8,128]{3,2,1,0:T(8,128)(2,1)S(1)} %get-tuple-element.54), channel_id=1, source_target_pairs={{0,1},{1,0},{2,3},{3,2},{4,5},{5,4},{6,7},{7,6},{8,9},{9,8},{10,11... | collective-permute-start | bytes 405512 | tf_op jit(solution)/shard_map/ppermute | solution.py:204
  88.2 8.7 %shard_map.88.image = bf16[4224,2048]{1,0:T(8,128)(2,1)S(1)} custom-call(s32[3]{0:T(128)S(1)} %pad_add_fusion.scalars, bf16[8,16,8,128]{3,2,1,0:T(8,128)(2,1)S(1)} %all-to-all-done.1.mine, bf16[8,16,8,128]{3,2,1,0:T(8,128)(2,1)S(1)} %collective-permute-done.17.theirs, bf16[33,128,128]{2,1,0:T(8,128)(2,1)S(1)} %bitcast.22), custom_call_target="tpu_custom_call" | custom-call | tf_op jit(solution)/shard_map/pallas_call | solution.py:117
  96.9 3.1 %shard_map.89 = (f32[8,8,2048]{2,1,0:T(8,128)S(1)}, bf16[8,8,2048]{2,1,0:T(8,128)(2,1)S(1)}) custom-call(s32[3]{0:T(128)S(1)} %pad_add_fusion.scalars, bf16[6,33,8,128]{3,2,1,0:T(8,128)(2,1)S(1)} %get-tuple-element.49.mine_a, bf16[2,33,8,128]{3,2,1,0:T(8,128)(2,1)S(1)} %get-tuple-element.52.mine_b, ...), custom_call_target="tpu_custom_call" | custom-call | tf_op jit(solution)/shard_map/pallas_call | solution.py:154
  100.0 0.1 collective-permute-start.18
  100.1 1.5 %collective-permute-done.18 = bf16[8,8,2048]{2,1,0:T(8,128)(2,1)S(1)} collective-permute-done((bf16[8,8,2048]{2,1,0:T(8,128)(2,1)S(1)}, bf16[8,8,2048]{2,1,0:T(8,128)(2,1)S(1)}, u32[]{:S(2)}, u32[]{:S(2)}) %collective-permute-start.18) | collective-permute-done | bytes 262176 | tf_op jit(solution)/shard_map/ppermute | solution.py:204
  101.7 16.6 %all_to_all.15 = bf16[8,8,2048]{2,1,0:T(8,128)(2,1)S(1)} all-to-all(bf16[8,8,2048]{2,1,0:T(8,128)(2,1)S(1)} %add_convert_fusion), channel_id=1, replica_groups=mesh['y'=4,'x'=4,'z'=8,'core'=2] {'z'}, dimensions={0} | all-to-all | bytes 524288 | tf_op jit(solution)/shard_map/all_to_all | solution.py:273
  118.3 0.7 convert_reduce_fusion
  (25 shorter events, 0.1 us)
Async XLA Ops:
  0.0 23.4 %copy-start = (bf16[528,528]{1,0:T(8,128)(2,1)S(1)}, bf16[528,528]{1,0:T(8,128)(2,1)}, u32[]{:S(2)}) copy-start(bf16[528,528]{1,0:T(8,128)(2,1)} %param.10) | copy-start | bytes 1672708
  0.8 7.1 %copy-start.2 = (bf16[1,16,8,128]{3,2,1,0:T(8,128)(2,1)S(1)}, bf16[1,16,8,128]{3,2,1,0:T(8,128)(2,1)}, u32[]{:S(2)}) copy-start(bf16[1,16,8,128]{3,2,1,0:T(8,128)(2,1)} %param.12) | copy-start | bytes 98308
  4.6 9.4 %collective-permute-start = (bf16[8,33,8,128]{3,2,1,0:T(8,128)(2,1)S(1)}, bf16[8,33,8,128]{3,2,1,0:T(8,128)(2,1)S(1)}, u32[]{:S(2)}, u32[]{:S(2)}) collective-permute-start(bf16[8,33,8,128]{3,2,1,0:T(8,128)(2,1)S(1)} %get-tuple-element.32), channel_id=1, source_target_pairs={{0,1},{1,0},{2,3},{3,2},{4,5},{5,4},{6,7},{7,6},{8,9},{9,8},{10,11... | collective-permute-start | bytes 1622024 | tf_op jit(solution)/shard_map/ppermute | solution.py:204
  8.8 14.5 %copy-start.3 = (s32[528]{0:T(1024)S(1)}, s32[528]{0:T(1024)}, u32[]{:S(2)}) copy-start(s32[528]{0:T(1024)} %param.15) | copy-start | bytes 6340
  8.8 28.0 %all-to-all-start = ((bf16[16,16,8,128]{3,2,1,0:T(8,128)(2,1)}), bf16[16,16,8,128]{3,2,1,0:T(8,128)(2,1)}, u32[]{:S(2)}, u32[]{:S(2)}) async-start(bf16[16,16,8,128]{3,2,1,0:T(8,128)(2,1)} %broadcast_in_dim.9), calls=%async_computation | async-start | bytes 1048576 | tf_op jit(solution)/shard_map/all_to_all | solution.py:234
  14.7 16.9 %collective-permute-start.1 = (bf16[66,8,128]{2,1,0:T(8,128)(2,1)S(1)}, bf16[66,8,128]{2,1,0:T(8,128)(2,1)S(1)}, u32[]{:S(2)}, u32[]{:S(2)}) collective-permute-start(bf16[66,8,128]{2,1,0:T(8,128)(2,1)S(1)} %get-tuple-element.34), channel_id=1, source_target_pairs={{0,8},{2,10},{4,12},{6,14},{8,0},{10,2},{12,4},{14,6},{1,9},{3,11}... | collective-permute-start | bytes 405512 | tf_op jit(solution)/shard_map/ppermute | solution.py:212
  21.7 3.4 %copy-start.4 = (s32[1,4]{1,0:T(1,128)S(1)}, s32[1,4]{1,0:T(1,128)}, u32[]{:S(2)}) copy-start(s32[1,4]{1,0:T(1,128)} %param.14) | copy-start | bytes 52
  21.7 15.1 %collective-permute-start.2 = (bf16[66,8,128]{2,1,0:T(8,128)(2,1)S(1)}, bf16[66,8,128]{2,1,0:T(8,128)(2,1)S(1)}, u32[]{:S(2)}, u32[]{:S(2)}) collective-permute-start(bf16[66,8,128]{2,1,0:T(8,128)(2,1)S(1)} %get-tuple-element.35), channel_id=1, source_target_pairs={{0,6},{2,8},{4,10},{6,12},{8,14},{10,0},{12,2},{14,4},{1,7},{3,9},... | collective-permute-start | bytes 405512 | tf_op jit(solution)/shard_map/ppermute | solution.py:212
  25.2 20.4 %collective-permute-start.3 = (bf16[66,8,128]{2,1,0:T(8,128)(2,1)S(1)}, bf16[66,8,128]{2,1,0:T(8,128)(2,1)S(1)}, u32[]{:S(2)}, u32[]{:S(2)}) collective-permute-start(bf16[66,8,128]{2,1,0:T(8,128)(2,1)S(1)} %get-tuple-element.36), channel_id=1, source_target_pairs={{0,10},{2,12},{4,14},{6,0},{8,2},{10,4},{12,6},{14,8},{1,11},{3,13... | collective-permute-start | bytes 405512 | tf_op jit(solution)/shard_map/ppermute | solution.py:212
  28.0 17.5 %collective-permute-start.4 = (bf16[66,8,128]{2,1,0:T(8,128)(2,1)S(1)}, bf16[66,8,128]{2,1,0:T(8,128)(2,1)S(1)}, u32[]{:S(2)}, u32[]{:S(2)}) collective-permute-start(bf16[66,8,128]{2,1,0:T(8,128)(2,1)S(1)} %get-tuple-element.37), channel_id=1, source_target_pairs={{0,4},{2,6},{4,8},{6,10},{8,12},{10,14},{12,0},{14,2},{1,5},{3,7},... | collective-permute-start | bytes 405512 | tf_op jit(solution)/shard_map/ppermute | solution.py:212
  29.2 16.4 %collective-permute-start.5 = (bf16[66,8,128]{2,1,0:T(8,128)(2,1)S(1)}, bf16[66,8,128]{2,1,0:T(8,128)(2,1)S(1)}, u32[]{:S(2)}, u32[]{:S(2)}) collective-permute-start(bf16[66,8,128]{2,1,0:T(8,128)(2,1)S(1)} %get-tuple-element.38), channel_id=1, source_target_pairs={{0,12},{2,14},{4,0},{6,2},{8,4},{10,6},{12,8},{14,10},{1,13},{3,15... | collective-permute-start | bytes 405512 | tf_op jit(solution)/shard_map/ppermute | solution.py:212
  31.6 15.2 %collective-permute-start.6 = (bf16[66,8,128]{2,1,0:T(8,128)(2,1)S(1)}, bf16[66,8,128]{2,1,0:T(8,128)(2,1)S(1)}, u32[]{:S(2)}, u32[]{:S(2)}) collective-permute-start(bf16[66,8,128]{2,1,0:T(8,128)(2,1)S(1)} %get-tuple-element.39), channel_id=1, source_target_pairs={{0,14},{2,0},{4,2},{6,4},{8,6},{10,8},{12,10},{14,12},{1,15},{3,1}... | collective-permute-start | bytes 405512 | tf_op jit(solution)/shard_map/ppermute | solution.py:212
  36.8 10.0 %collective-permute-start.7 = (bf16[66,8,128]{2,1,0:T(8,128)(2,1)S(1)}, bf16[66,8,128]{2,1,0:T(8,128)(2,1)S(1)}, u32[]{:S(2)}, u32[]{:S(2)}) collective-permute-start(bf16[66,8,128]{2,1,0:T(8,128)(2,1)S(1)} %get-tuple-element.40), channel_id=1, source_target_pairs={{0,2},{2,4},{4,6},{6,8},{8,10},{10,12},{12,14},{14,0},{1,3},{3,5},... | collective-permute-start | bytes 405512 | tf_op jit(solution)/shard_map/ppermute | solution.py:212
  38.8 41.8 %all-to-all-start.1 = ((bf16[8,16,8,128]{3,2,1,0:T(8,128)(2,1)}), bf16[8,16,8,128]{3,2,1,0:T(8,128)(2,1)S(1)}, u32[]{:S(2)}, u32[]{:S(2)}) async-start(bf16[8,16,8,128]{3,2,1,0:T(8,128)(2,1)} %broadcast_in_dim.10), calls=%async_computation.1 | async-start | bytes 524288 | tf_op jit(solution)/shard_map/all_to_all | solution.py:251
  46.8 1.1 copy-start.5
  49.3 38.9 %copy-start.1 = (bf16[1,33,128,128]{3,2,1,0:T(8,128)(2,1)S(1)}, bf16[1,33,128,128]{3,2,1,0:T(8,128)(2,1)}, u32[]{:S(2)}) copy-start(bf16[1,33,128,128]{3,2,1,0:T(8,128)(2,1)} %param.11) | copy-start | bytes 3244036
  50.6 13.6 %collective-permute-start.8 = (bf16[66,8,128]{2,1,0:T(8,128)(2,1)S(1)}, bf16[66,8,128]{2,1,0:T(8,128)(2,1)S(1)}, u32[]{:S(2)}, u32[]{:S(2)}) collective-permute-start(bf16[66,8,128]{2,1,0:T(8,128)(2,1)S(1)} %get-tuple-element.44), channel_id=1, source_target_pairs={{0,8},{2,10},{4,12},{6,14},{8,0},{10,2},{12,4},{14,6},{1,9},{3,11}... | collective-permute-start | bytes 405512 | tf_op jit(solution)/shard_map/ppermute | solution.py:212
  54.7 9.4 %collective-permute-start.9 = (bf16[66,8,128]{2,1,0:T(8,128)(2,1)S(1)}, bf16[66,8,128]{2,1,0:T(8,128)(2,1)S(1)}, u32[]{:S(2)}, u32[]{:S(2)}) collective-permute-start(bf16[66,8,128]{2,1,0:T(8,128)(2,1)S(1)} %get-tuple-element.45), channel_id=1, source_target_pairs={{0,6},{2,8},{4,10},{6,12},{8,14},{10,0},{12,2},{14,4},{1,7},{3,9},... | collective-permute-start | bytes 405512 | tf_op jit(solution)/shard_map/ppermute | solution.py:212
  55.6 14.5 %collective-permute-start.10 = (bf16[66,8,128]{2,1,0:T(8,128)(2,1)S(1)}, bf16[66,8,128]{2,1,0:T(8,128)(2,1)S(1)}, u32[]{:S(2)}, u32[]{:S(2)}) collective-permute-start(bf16[66,8,128]{2,1,0:T(8,128)(2,1)S(1)} %get-tuple-element.46), channel_id=1, source_target_pairs={{0,10},{2,12},{4,14},{6,0},{8,2},{10,4},{12,6},{14,8},{1,11},{3,13... | collective-permute-start | bytes 405512 | tf_op jit(solution)/shard_map/ppermute | solution.py:212
  59.2 13.2 %collective-permute-start.11 = (bf16[66,8,128]{2,1,0:T(8,128)(2,1)S(1)}, bf16[66,8,128]{2,1,0:T(8,128)(2,1)S(1)}, u32[]{:S(2)}, u32[]{:S(2)}) collective-permute-start(bf16[66,8,128]{2,1,0:T(8,128)(2,1)S(1)} %get-tuple-element.47), channel_id=1, source_target_pairs={{0,4},{2,6},{4,8},{6,10},{8,12},{10,14},{12,0},{14,2},{1,5},{3,7},... | collective-permute-start | bytes 405512 | tf_op jit(solution)/shard_map/ppermute | solution.py:212
  59.5 18.2 %collective-permute-start.12 = (bf16[66,8,128]{2,1,0:T(8,128)(2,1)S(1)}, bf16[66,8,128]{2,1,0:T(8,128)(2,1)S(1)}, u32[]{:S(2)}, u32[]{:S(2)}) collective-permute-start(bf16[66,8,128]{2,1,0:T(8,128)(2,1)S(1)} %get-tuple-element.48), channel_id=1, source_target_pairs={{0,12},{2,14},{4,0},{6,2},{8,4},{10,6},{12,8},{14,10},{1,13},{3,15... | collective-permute-start | bytes 405512 | tf_op jit(solution)/shard_map/ppermute | solution.py:212
  78.3 18.6 %collective-permute-start.15 = (bf16[6,33,8,128]{3,2,1,0:T(8,128)(2,1)S(1)}, bf16[6,33,8,128]{3,2,1,0:T(8,128)(2,1)S(1)}, u32[]{:S(2)}, u32[]{:S(2)}) collective-permute-start(bf16[6,33,8,128]{3,2,1,0:T(8,128)(2,1)S(1)} %get-tuple-element.53), channel_id=1, source_target_pairs={{0,1},{1,0},{2,3},{3,2},{4,5},{5,4},{6,7},{7,6},{8,9},{9,8},{10,11... | collective-permute-start | bytes 1216520 | tf_op jit(solution)/shard_map/ppermute | solution.py:204
  79.1 5.3 %collective-permute-start.13 = (bf16[66,8,128]{2,1,0:T(8,128)(2,1)}, bf16[66,8,128]{2,1,0:T(8,128)(2,1)S(1)}, u32[]{:S(2)}, u32[]{:S(2)}) collective-permute-start(bf16[66,8,128]{2,1,0:T(8,128)(2,1)} %get-tuple-element.50), channel_id=1, source_target_pairs={{0,14},{2,0},{4,2},{6,4},{8,6},{10,8},{12,10},{14,12},{1,15},{3,1}... | collective-permute-start | bytes 405512 | tf_op jit(solution)/shard_map/ppermute | solution.py:212
  80.1 6.2 %collective-permute-start.14 = (bf16[66,8,128]{2,1,0:T(8,128)(2,1)}, bf16[66,8,128]{2,1,0:T(8,128)(2,1)S(1)}, u32[]{:S(2)}, u32[]{:S(2)}) collective-permute-start(bf16[66,8,128]{2,1,0:T(8,128)(2,1)} %get-tuple-element.51), channel_id=1, source_target_pairs={{0,2},{2,4},{4,6},{6,8},{8,10},{10,12},{12,14},{14,0},{1,3},{3,5},... | collective-permute-start | bytes 405512 | tf_op jit(solution)/shard_map/ppermute | solution.py:212
  80.6 7.6 %collective-permute-start.17 = (bf16[8,16,8,128]{3,2,1,0:T(8,128)(2,1)S(1)}, bf16[8,16,8,128]{3,2,1,0:T(8,128)(2,1)S(1)}, u32[]{:S(2)}, u32[]{:S(2)}) collective-permute-start(bf16[8,16,8,128]{3,2,1,0:T(8,128)(2,1)S(1)} %all-to-all-done.1.mine), channel_id=1, source_target_pairs={{0,1},{1,0},{2,3},{3,2},{4,5},{5,4},{6,7},{7,6},{8,9},{9,8},{10,11... | collective-permute-start | bytes 786440 | tf_op jit(solution)/shard_map/ppermute | solution.py:204
  86.9 10.1 %collective-permute-start.16 = (bf16[2,33,8,128]{3,2,1,0:T(8,128)(2,1)S(1)}, bf16[2,33,8,128]{3,2,1,0:T(8,128)(2,1)S(1)}, u32[]{:S(2)}, u32[]{:S(2)}) collective-permute-start(bf16[2,33,8,128]{3,2,1,0:T(8,128)(2,1)S(1)} %get-tuple-element.54), channel_id=1, source_target_pairs={{0,1},{1,0},{2,3},{3,2},{4,5},{5,4},{6,7},{7,6},{8,9},{9,8},{10,11... | collective-permute-start | bytes 405512 | tf_op jit(solution)/shard_map/ppermute | solution.py:204
  100.0 1.6 %collective-permute-start.18 = (bf16[8,8,2048]{2,1,0:T(8,128)(2,1)S(1)}, bf16[8,8,2048]{2,1,0:T(8,128)(2,1)S(1)}, u32[]{:S(2)}, u32[]{:S(2)}) collective-permute-start(bf16[8,8,2048]{2,1,0:T(8,128)(2,1)S(1)} %get-tuple-element.56), channel_id=1, source_target_pairs={{0,1},{1,0},{2,3},{3,2},{4,5},{5,4},{6,7},{7,6},{8,9},{9,8},{10,11... | collective-permute-start | bytes 786440 | tf_op jit(solution)/shard_map/ppermute | solution.py:204
